TPU v7x, 32 devices: a whole 2x2x4 slice. The times are simulated.
32 devices in a mesh: mem: 8 (over y, x, core), lat: 4 (over z).
Axes of the slice: x: 2, y: 2, z: 4, core: 2. Of those that a mesh axis runs over, the one named last changes fastest.
Arguments:
- state: float32 [8, 641, 8, 160], P('mem', None, 'lat'), may hold values from -6 to 6
- conv_kernel: float32 [25, 641], replicated, may hold values from -1.25 to 1.25
- norm_gain: float32 [641], replicated, may hold values from 0.5 to 1.5
- up_weight: bfloat16 [641, 1282], replicated, may hold values from -0.25 to 0.25
- down_weight: bfloat16 [1282, 641], replicated, may hold values from -0.15625 to 0.15625
- field_head_weight: bfloat16 [641, 72], replicated, may hold values from -0.25 to 0.25
- target: float32 [72, 8, 160], P(None, 'lat'), may hold values from -9 to 9
- field_weight: float32 [72], replicated, may hold values from 0.3 to 3
Outputs:
- loss: float32 [], replicated
- grad_kernel: float32 [25, 641], replicated
- grad_gain: float32 [641], replicated
- grad_up: float32 [641, 1282], replicated
- grad_down: float32 [1282, 641], replicated
- grad_head: float32 [641, 72], replicated
All inputs are finite; a program needn't handle non-finite values.
Results may differ from a plain program's by a relative error of at most 0.005.
The roundings to bfloat16 on the way count: a program that leaves them out, or rounds other values in their place, can miss the bound.
Values may be sent and summed in bfloat16 or wider, within the bound.
No kernel may reach another device: no remote copies, remote signals or barrier semaphores. Data moves between devices by JAX's collectives and lax.ppermute only.
A program may use at most 128 MiB of HBM per device.

v0:
```python
import functools
import math

import jax
import jax.numpy as jnp
from jax import lax
from jax.experimental import pallas as pl
from jax.experimental.pallas import tpu as pltpu
from jax.sharding import PartitionSpec as P


DELTA = 0.1
EPSILON = 1e-05
BF = jnp.bfloat16
F32 = jnp.float32


def dot(left, right, dims):
    return lax.dot_general(left, right, (dims, ((), ())), preferred_element_type=F32)


def swap(value, axis, mask):
    count = lax.axis_size(axis)
    return lax.ppermute(value, axis, [(i, i ^ mask) for i in range(count)])


def stages():
    members = lax.axis_size("mem")
    return (("mem", 1, 2), ("mem", 2, members // 2), ("lat", 1, lax.axis_size("lat")))


def order(size):
    return sorted(range(1, size), key=lambda k: -bin(k).count("1"))


def place_on(stage):
    axis, stride, size = stage
    return (lax.axis_index(axis) // stride) % size


def hand_out(stage, pieces_ref, own_ref, sent_refs):
    place = place_on(stage)
    own_ref[...] = pieces_ref[place]
    for k, ref in zip(order(stage[2]), sent_refs):
        ref[...] = pieces_ref[lax.bitwise_xor(place, k)].astype(ref.dtype)


def sum_kernel(stage, counts, *refs):
    totals = []
    for count in counts:
        total = refs[0][...]
        for ref in refs[1:count]:
            total = total + ref[...].astype(F32)
        totals.append(total)
        refs = refs[count:]
    if stage is None:
        refs[0][...] = totals[0].astype(BF)
        return
    size = stage[2]
    own_ref, *sent_refs, pieces_ref = refs
    rows = totals[0].shape[0] // size
    for n, total in enumerate(totals):
        for j in range(size):
            pieces_ref[j, n * rows : (n + 1) * rows] = total[j * rows : (j + 1) * rows]
    hand_out(stage, pieces_ref, own_ref, sent_refs)


def sum_up(groups, stage):
    length, columns = groups[0][0].shape
    if stage is None:
        outs, scratch = [shape((length, columns), BF)], []
    else:
        rows = length // stage[2] * len(groups)
        outs = [shape((rows, columns))] + [shape((rows, columns), BF)] * (stage[2] - 1)
        scratch = [pltpu.VMEM((stage[2], rows, columns), F32)]
    kernel = functools.partial(sum_kernel, stage, [len(g) for g in groups])
    return call(kernel, outs, sum(groups, ()), length * columns * 4, scratch)


def send(stage, pieces):
    axis, stride, size = stage
    return [swap(p, axis, k * stride) for k, p in zip(order(size), pieces)]


def place_kernel(stage, own_ref, *refs):
    place = place_on(stage)
    out_ref = refs[-1]
    out_ref[place] = own_ref[...]
    for k, ref in zip(order(stage[2]), refs[:-1]):
        out_ref[lax.bitwise_xor(place, k)] = ref[...]


def collect(value, got, stage):
    rows, columns = value.shape
    kernel = functools.partial(place_kernel, stage)
    (out,) = call(kernel, [shape((stage[2], rows, columns), BF)], (value, *got), rows * columns)
    return out.reshape(stage[2] * rows, columns)


def scatter_start(own, sent):
    core, plane, _ = stages()
    return sum_up([(own, *send(core, [sent]))], plane)


def across_plane(own, *sent):
    return (own, *send(stages()[1], sent))


def finish_exchange(group):
    core, plane, line = stages()
    own, *sent = sum_up([group], line)
    got = send(line, sent)
    value = sum_up([(own, *got)], None)[0]
    for stage in (line, plane):
        got = send(stage, [value] * (stage[2] - 1))
        value = collect(value, got, stage)
    return value, send(core, [value])[0]


def call(kernel, outs, args, flops, scratch=()):
    spec = pl.BlockSpec(memory_space=pltpu.VMEM)
    size = sum(math.prod(o.shape) * o.dtype.itemsize for o in outs)
    size += sum(math.prod(a.shape) * a.dtype.itemsize for a in args)
    return pl.pallas_call(
        kernel,
        out_shape=outs,
        in_specs=[spec] * len(args),
        out_specs=[spec] * len(outs),
        scratch_shapes=list(scratch),
        cost_estimate=pl.CostEstimate(flops=flops, bytes_accessed=size, transcendentals=0),
        compiler_params=pltpu.CompilerParams(vmem_limit_bytes=30 * 1024 * 1024),
    )(*args)


def shape(dims, dtype=F32):
    return jax.ShapeDtypeStruct(tuple(dims), dtype)


def spans(total, step):
    count = max(total // step, 1)
    return [(n * step, total if n == count - 1 else (n + 1) * step) for n in range(count)]


def pack_kernel(field_ref, out_ref):
    rows, width, channels = field_ref.shape
    lanes = out_ref.shape[1]
    cells = rows * width
    for r in range(rows):
        out_ref[r * width : (r + 1) * width, :] = field_ref[r, :, :lanes]
    last = jnp.concatenate(
        [
            jnp.broadcast_to(field_ref[r, :, lanes:channels], (width, 128))
            for r in range(rows)
        ]
    )
    out_ref[cells : cells + 8, :] = jnp.zeros((8, lanes), F32)
    out_ref[cells : cells + 8, :cells] = last.T[:8]


def fill(win_ref, row, main, last):
    width = main.shape[0]
    lanes = main.shape[1]
    channels = win_ref.shape[2]
    for columns, value in ((slice(0, lanes), main), (slice(lanes, channels), last)):
        win_ref[row, 8 : 8 + width, columns] = value
        win_ref[row, 6:8, columns] = value[width - 2 :]
        win_ref[row, 8 + width : 10 + width, columns] = value[:2]


def convolve(win_ref, kernel_ref, rows, sum_in_ref, sum_ref, first_row, height, width):
    lanes = kernel_ref.shape[1] // 128 * 128
    part = width // 2

    def block(columns):
        for half in range(2):
            first = half * part
            spans = [slice(i * width + first, i * width + first + part) for i in range(height)]
            acc = [
                win_ref[i + 2 - first_row, 8 + first : 8 + first + part, columns]
                if sum_in_ref is None
                else sum_in_ref[spans[i], columns]
                for i in range(height)
            ]
            for w in rows:
                for b in range(5):
                    at = 6 + b + first
                    moved = win_ref[w - first_row, at : at + part, columns]
                    for i in range(height):
                        if 0 <= w - i < 5:
                            t = 5 * (w - i) + b
                            acc[i] = acc[i] + kernel_ref[t : t + 1, columns] * moved
            for i in range(height):
                sum_ref[spans[i], columns] = acc[i]

    @pl.loop(0, lanes // 128)
    def _(n):
        block(pl.ds(pl.multiple_of(n * 128, 128), 128))

    block(slice(lanes, kernel_ref.shape[1]))


def prep_kernel(
    bands, field_ref, kernel_ref, gain_in_ref, target_ref, field_weight_ref, early_up_ref,
    early_head_ref, part_ref, gain_ref, truth_ref, weight_ref, win_ref, turn_ref,
):
    height, width, channels = field_ref.shape
    lanes = channels // 128 * 128
    fields, _ = truth_ref.shape
    for r in range(height):
        fill(win_ref, r, field_ref[r, :, :lanes], field_ref[r, :, lanes:])
    convolve(win_ref, kernel_ref, range(2, 2 + height), None, part_ref, 2, height, width)
    gain_ref[...] = gain_in_ref[...][None, :]
    turn_ref[...] = jnp.zeros_like(turn_ref)
    turn_ref[:1, :fields] = field_weight_ref[...][None, :]
    column = turn_ref[...].T[:fields, :1]
    base = (lax.axis_index("lat") * height).astype(F32)
    for r in range(height):
        truth_ref[:, r * width : (r + 1) * width] = target_ref[:, r, :]
        row = jnp.full((1, width), r, F32) + base
        area = jnp.cos(0.5 * math.pi * ((row + 0.5) / (bands * height) - 1.0))
        weight_ref[:, r * width : (r + 1) * width] = column * area


def forward_kernel(
    field_ref, part_ref, first_ref, second_ref, kernel_ref, gain_ref, up_ref, down_ref, head_ref,
    truth_ref, forecast_ref, miss_ref, win_ref, normed_ref, inverse_ref, scaled_ref, turned_ref, hidden_ref,
    slope_ref, rounded_ref, summed_ref,
):
    height, width, channels = field_ref.shape
    lanes = first_ref.shape[1]
    cells = height * width

    odd = lax.axis_index("lat") % 2 == 1
    for base, odds_ref, evens_ref in (
        (0, first_ref, second_ref), (2 + height, second_ref, first_ref)
    ):
        rows = jnp.where(odd, odds_ref[...], evens_ref[...])
        turned = rows[2 * width : 2 * width + 8, :].T
        for r in range(2):
            span = slice(r * width, (r + 1) * width)
            fill(win_ref, base + r, rows[span, :], turned[span, :1])
    for r in range(height):
        fill(win_ref, 2 + r, field_ref[r, :, :lanes], field_ref[r, :, lanes:])
    rows = [w for w in range(height + 4) if not 2 <= w < 2 + height]
    convolve(win_ref, kernel_ref, rows, part_ref, summed_ref, 0, height, width)
    part = width // 2
    for start in range(0, cells, part):
        rows = slice(start, start + part)
        summed = summed_ref[rows, :]
        center = summed - jnp.sum(summed, axis=1, keepdims=True) * (1.0 / channels)
        variance = jnp.sum(center * center, axis=1, keepdims=True) * (1.0 / channels)
        inverse = lax.rsqrt(variance + EPSILON)
        normed = center * inverse
        normed_ref[rows, :] = normed
        inverse_ref[rows, :] = inverse
        scaled_ref[rows, :] = (normed * gain_ref[...]).astype(BF)

    turned_ref[...] = scaled_ref[...].T
    for lo, hi in spans(up_ref.shape[1], 256):
        preact = dot(scaled_ref[...], up_ref[:, lo:hi], ((1,), (0,)))
        cumul = 0.5 * (1.0 + lax.erf(preact * (1.0 / math.sqrt(2.0))))
        density = jnp.exp(-0.5 * preact * preact) * (1.0 / math.sqrt(2.0 * math.pi))
        hidden = (preact * cumul).astype(BF)
        hidden_ref[:, lo:hi] = hidden
        slope_ref[:, lo:hi] = cumul + preact * density
        summed_ref[...] += dot(hidden, down_ref[:, lo:hi], ((1,), (1,)))
    rounded = summed_ref[...].astype(BF)
    rounded_ref[...] = rounded
    forecast = dot(head_ref[...], rounded, ((1,), (1,)))
    forecast_ref[...] = forecast
    miss_ref[...] = forecast - truth_ref[...]


def score_kernel(members, bands, count, *refs):
    other_refs = refs[: members - 1]
    (
        forecast_ref, miss_ref, weight_ref, head_ref, down_ref, rounded_ref, hidden_ref, slope_ref,
        turned_ref, own_ref, sent_ref, output_ref, preact_ref, head_term_ref, factor_ref, loss_ref,
        cot_ref, main_ref,
    ) = refs[members - 1 :]
    fields, cells = forecast_ref.shape
    lanes = own_ref.shape[1]
    mine = lax.axis_index("mem") * bands + lax.axis_index("lat")
    forecast = forecast_ref[...]
    weights = weight_ref[...]
    miss = miss_ref[...]
    pair_abs = jnp.zeros_like(forecast)
    pair_der = jnp.zeros_like(forecast)
    for ref in other_refs:
        diff = forecast - ref[...]
        square = diff * diff + DELTA * DELTA
        inverse = lax.rsqrt(square)
        pair_abs = pair_abs + (square * inverse - DELTA)
        pair_der = pair_der + diff * inverse
    square = miss * miss + DELTA * DELTA
    inverse = lax.rsqrt(square)
    spread = (square * inverse - DELTA) * (1.0 / members) - pair_abs * (
        1.0 / (2.0 * members * (members - 1))
    )
    part = jnp.sum(jnp.sum(weights * spread, axis=1, keepdims=True), axis=0, keepdims=True)
    first = part.astype(BF).astype(F32)
    second = (part - first).astype(BF).astype(F32)
    third = part - first - second
    slot = lax.broadcasted_iota(jnp.int32, (8, lanes), 1) == mine
    line = lax.broadcasted_iota(jnp.int32, (8, lanes), 0)
    value = jnp.where(line == 0, first, jnp.where(line == 1, second, third))
    loss_ref[...] = jnp.where(slot & (line < 3), value, 0.0)
    cot = (
        weights
        * (miss * inverse - pair_der * (1.0 / (members - 1)))
        * (1.0 / (members * math.sqrt(count)))
    )
    co = cot.astype(BF)
    cot_ref[...] = jnp.zeros_like(cot_ref)
    cot_ref[:fields, :cells] = co.astype(F32)
    turned = cot_ref[...].T[:cells, :fields].astype(BF)
    head_term_ref[...] = dot(co, rounded_ref[...], ((1,), (0,)))
    d_output = dot(turned, head_ref[...], ((1,), (0,)))
    output_ref[...] = d_output
    d_round = d_output.astype(BF)
    for lo, hi in spans(down_ref.shape[1], 256):
        factor_ref[:, lo:hi] = dot(co, hidden_ref[:, lo:hi], ((1,), (0,)))
        d_hidden = dot(d_round, down_ref[:, lo:hi], ((1,), (0,)))
        preact_ref[:, lo:hi] = (d_hidden * slope_ref[:, lo:hi]).astype(BF)
    gradient_rows(main_ref, 0, main_ref.shape[0] * main_ref.shape[1], turned_ref, preact_ref)
    hand_out(stages()[0], main_ref, own_ref, [sent_ref])


def gradient_rows(out_ref, first, count, turned_ref, preact_ref):
    piece, lanes = out_ref.shape[1:]
    done = 0
    while done < count:
        h, r = (first + done) // lanes, (first + done) % lanes
        p, at = done // piece, done % piece
        take = min(lanes - r, piece - at, count - done)
        out_ref[p, at : at + take, :] = dot(
            turned_ref[r : r + take, :], preact_ref[:, h * lanes : (h + 1) * lanes], ((1,), (0,))
        )
        done += take


def rest_kernel(
    preact_ref, turned_ref, scaled_ref, up_ref, gain_ref, normed_ref, inverse_ref, output_ref,
    win_ref, head_term_ref, factor_ref, loss_ref, after_ref,
    own_ref, sent_ref, wide_ref, grads_ref, heads_ref, pieces_ref,
):
    cells, channels = normed_ref.shape
    hidden_units = preact_ref.shape[1]
    fields = head_term_ref.shape[0]
    size, piece, lanes = pieces_ref.shape
    halves = hidden_units // lanes
    even = halves * lanes
    height = win_ref.shape[0] - 4
    width = cells // height
    base = size * piece - 256
    gradient_rows(pieces_ref, halves * lanes - base, base, turned_ref, preact_ref)
    out_ref = pieces_ref.at[size - 1]
    base -= (size - 1) * piece
    for h in range(halves):
        at = base + h * fields
        out_ref[at : at + fields, :] = factor_ref[:, h * lanes : (h + 1) * lanes]
    at = base + halves * fields
    out_ref[at : at + fields, :] = head_term_ref[:, :lanes]
    at += fields

    d_scaled = dot(preact_ref[...], up_ref[...], ((1,), (1,)))
    normed = normed_ref[...]
    grads_ref[...] = jnp.zeros_like(grads_ref)
    grads_ref[25:26, :channels] = jnp.sum(d_scaled * normed, axis=0, keepdims=True)
    d_normed = d_scaled * gain_ref[...]
    d_summed = output_ref[...] + inverse_ref[...] * (
        d_normed
        - jnp.sum(d_normed, axis=1, keepdims=True) * (1.0 / channels)
        - normed * (jnp.sum(d_normed * normed, axis=1, keepdims=True) * (1.0 / channels))
    )
    wide_ref[...] = d_summed

    def correlate(columns):
        for a in range(5):
            for b in range(5):
                total = None
                for i in range(height):
                    term = jnp.sum(
                        wide_ref[i * width : (i + 1) * width, columns]
                        * win_ref[i + a, 6 + b : 6 + b + width, columns],
                        axis=0,
                        keepdims=True,
                    )
                    total = term if total is None else total + term
                t = 5 * a + b
                grads_ref[t : t + 1, columns] = total

    @pl.loop(0, lanes // 128)
    def _(n):
        correlate(pl.ds(pl.multiple_of(n * 128, 128), 128))

    correlate(slice(lanes, channels))

    out_ref[at : at + 26, :] = grads_ref[:26, :lanes]
    at += 26
    last = dot(turned_ref[lanes - 7 : channels, :], preact_ref[...], ((1,), (0,)))[7:8]
    for h in range(halves):
        out_ref[at + h : at + h + 1, :] = last[:, h * lanes : (h + 1) * lanes]
    at += halves
    left = hidden_units - even
    columns = dot(preact_ref[:, even:], scaled_ref[...], ((0,), (0,)))
    out_ref[at : at + left, :] = columns[:, :lanes]
    at += left
    out_ref[at:, :] = jnp.zeros((out_ref.shape[0] - at, lanes), F32)
    heads_ref[...] = jnp.zeros_like(heads_ref)
    heads_ref[:fields, :left] = factor_ref[:, even:]
    out_ref[at : at + left, :128] = heads_ref[...].T[:left]
    at += left
    heads_ref[:fields, :1] = head_term_ref[:, lanes:]
    out_ref[at : at + 1, :128] = heads_ref[...].T[:1]
    at += 1
    out_ref[at : at + 1, :128] = grads_ref[:, lanes : lanes + 128].T[:1]
    at += 1
    out_ref[at : at + 1, :left] = last[:, even:]
    at += 1
    out_ref[at : at + 3, :] = loss_ref[:3]
    hand_out(stages()[0], pieces_ref, own_ref, [sent_ref])


def finish_kernel(
    count, own_one_ref, got_one_ref, own_two_ref, got_two_ref, head_ref,
    loss_ref, kernel_ref, gain_ref, up_ref, down_ref, head_out_ref, one_ref, two_ref,
):
    core = place_on(stages()[0])
    for out, own, got in (
        (one_ref, own_one_ref, got_one_ref), (two_ref, own_two_ref, got_two_ref)
    ):
        out[core] = own[...].astype(F32)
        out[1 - core] = got[...].astype(F32)
    channels, hidden_units = up_ref.shape
    lanes = one_ref.shape[2]
    fields = head_ref.shape[1]
    taps = kernel_ref.shape[0]
    halves = hidden_units // lanes
    even = halves * lanes
    left = hidden_units - even
    rows = 0
    for ref in (one_ref.at[0], one_ref.at[1], two_ref.at[0], two_ref.at[1]):
        at = 0
        while at < ref.shape[0] and rows < even:
            h, r = rows // lanes, rows % lanes
            take = min(lanes - r, ref.shape[0] - at, even - rows)
            up_ref[r : r + take, h * lanes : (h + 1) * lanes] = ref[at : at + take, :]
            rows += take
            at += take
    extra = two_ref.at[1][two_ref.shape[1] - 256 :, :]
    for h in range(halves):
        down_ref[:, h * lanes : (h + 1) * lanes] = dot(
            head_ref[...], extra[h * fields : (h + 1) * fields, :].astype(BF), ((1,), (0,))
        )
    at = halves * fields
    head_out_ref[:, :lanes] = extra[at : at + fields]
    at += fields
    kernel_ref[:, :lanes] = extra[at : at + taps]
    at += taps
    gain_ref[:, :lanes] = extra[at : at + 1]
    at += 1
    for h in range(halves):
        up_ref[lanes:channels, h * lanes : (h + 1) * lanes] = extra[at + h : at + h + 1]
    at += halves
    tail = extra[240:256].T
    up_ref[:lanes, even:] = tail[:lanes, at - 240 : at - 240 + left]
    at += left
    down_ref[:, even:] = dot(
        head_ref[...], extra[at : at + left, :fields].astype(BF), ((1,), (1,))
    )
    at += left
    head_out_ref[:, lanes:] = tail[:fields, at - 240 : at - 239]
    at += 1
    kernel_ref[:, lanes:] = tail[:taps, at - 240 : at - 239]
    gain_ref[:, lanes:] = extra[at : at + 1, taps : taps + 1]
    at += 1
    up_ref[lanes:channels, even:] = extra[at : at + 1, :left]
    at += 1
    total = extra[at : at + 1] + extra[at + 1 : at + 2] + extra[at + 2 : at + 3]
    loss_ref[...] = jnp.sum(total, axis=1, keepdims=True) * (1.0 / count)


def local(
    state, conv_kernel, norm_gain, up_weight, down_weight, field_head_weight, target, field_weight
):
    members = lax.axis_size("mem")
    bands = lax.axis_size("lat")
    field = jnp.transpose(state[0], (1, 2, 0))
    height, width, channels = field.shape
    cells = height * width
    hidden_units = up_weight.shape[1]
    nlat = bands * height
    nfields = target.shape[0]
    lanes = channels // 128 * 128
    halves = hidden_units // lanes
    down_turned = down_weight.T
    head_turned = field_head_weight.T

    odd = lax.axis_index("lat") % 2

    def packed(first):
        return call(
            pack_kernel, [shape((2 * width + 8, lanes))], (field[first : first + 2],), 1000000
        )[0]

    def trade(value, start):
        pairs = [(i, i + 1) for i in range(start, bands - 1, 2)]
        return lax.ppermute(value, "lat", pairs + [(j, i) for i, j in pairs])

    head = packed(0)
    tail = head if height == 2 else packed(height - 2)
    if height == 2:
        traded = [trade(head, 0), trade(head, 1)]
    else:
        traded = [
            trade(jnp.where(odd == 0, tail, head), 0), trade(jnp.where(odd == 0, head, tail), 1)
        ]
    count = nlat * width * nfields
    part, gain, truth, weights = call(
        functools.partial(prep_kernel, bands),
        [
            shape((cells, channels)),
            shape((1, channels)),
            shape((nfields, cells)),
            shape((nfields, cells)),
        ],
        (field, conv_kernel, norm_gain, target, field_weight, up_weight, head_turned),
        10**8,
        [pltpu.VMEM((height, width + 16, channels), F32), pltpu.VMEM((128, 128), F32)],
    )
    mlp = 2 * cells * channels * hidden_units
    forecast, miss, window, normed, inverse, scaled, turned, hidden, slope, rounded = call(
        forward_kernel,
        [
            shape((nfields, cells)),
            shape((nfields, cells)),
            shape((height + 4, width + 16, channels)),
            shape((cells, channels)),
            shape((cells, 1)),
            shape((cells, channels), BF),
            shape((channels, cells), BF),
            shape((cells, hidden_units), BF),
            shape((cells, hidden_units)),
            shape((cells, channels), BF),
        ],
        (
            field, part, *traded, conv_kernel, gain, up_weight, down_turned, head_turned,
            truth,
        ),
        2 * mlp,
        [pltpu.VMEM((cells, channels), F32)],
    )
    near = [forecast] + [swap(forecast, "mem", 2 * k) for k in order(members // 2)]
    others = near[1:] + [swap(piece, "mem", 1) for piece in near]
    main_rows = halves * lanes
    half = (main_rows + 256) // 4
    small_half = half
    own, sent, d_output, d_preact, head_term, factor, loss_rows = call(
        functools.partial(score_kernel, members, bands, count),
        [
            shape((half, lanes)),
            shape((half, lanes)),
            shape((cells, channels)),
            shape((cells, hidden_units), BF),
            shape((nfields, channels)),
            shape((nfields, hidden_units)),
            shape((8, lanes)),
        ],
        (
            *others, forecast, miss, weights, head_turned, down_turned, rounded, hidden, slope,
            turned,
        ),
        2 * mlp,
        [
            pltpu.VMEM((128, -(-cells // 128) * 128), F32),
            pltpu.VMEM((2, half, lanes), F32),
        ],
    )
    one = scatter_start(own, sent)
    first = across_plane(*one)
    own, sent = call(
        rest_kernel,
        [shape((small_half, lanes)), shape((small_half, lanes))],
        (
            d_preact, turned, scaled, up_weight, gain, normed, inverse, d_output, window,
            head_term, factor, loss_rows, one[0],
        ),
        2 * mlp,
        [
            pltpu.VMEM((cells, channels), F32),
            pltpu.VMEM((128, lanes + 128), F32),
            pltpu.VMEM((128, 128), F32),
            pltpu.VMEM((2, small_half, lanes), F32),
        ],
    )
    two = scatter_start(own, sent)
    second = across_plane(*two)
    one = finish_exchange(first)
    two = finish_exchange(second)
    loss, grad_kernel, grad_gain, grad_up, grad_down, grad_head = call(
        functools.partial(finish_kernel, count),
        [
            shape((1, 1)),
            shape(conv_kernel.shape),
            shape((1, channels)),
            shape(up_weight.shape),
            shape((channels, hidden_units)),
            shape((nfields, channels)),
        ],
        (*one, *two, field_head_weight),
        mlp // 4,
        [pltpu.VMEM((2, half, lanes), F32), pltpu.VMEM((2, small_half, lanes), F32)],
    )
    return (
        loss.reshape(()), grad_kernel, grad_gain[0], grad_up, grad_down.T, grad_head.T,
    )


def solution(mesh):
    return jax.shard_map(
        local,
        mesh=mesh,
        in_specs=(P("mem", None, "lat", None), P(), P(), P(), P(), P(), P(None, "lat", None), P()),
        out_specs=(P(), P(), P(), P(), P(), P()),
        check_vma=False,
    )
```

profile of v0, /device:TPU:0, one launch (start us, length us, event | category | flops | bytes accessed | tf_op | source)
XLA Modules:
  0.0 111.8 jit_solution(12702502659027956359)
XLA Ops:
  0.7 1.3 %copy-done.2 = f32[1,641,2,160]{1,3,2,0:T(8,128)S(1)} copy-done((f32[1,641,2,160]{1,3,2,0:T(8,128)S(1)}, f32[1,641,2,160]{1,3,2,0:T(8,128)}, u32[]{:S(2)}) %copy-start.2) | copy-done | bytes 820504
  2.0 0.2 shard_map.128
  2.1 3.1 %collective-permute-start = (f32[328,640]{1,0:T(8,128)S(1)}, f32[328,640]{1,0:T(8,128)S(1)}, u32[]{:S(2)}, u32[]{:S(2)}) collective-permute-start(f32[328,640]{1,0:T(8,128)S(1)} %shard_map.128), channel_id=1, source_target_pairs={{0,1},{2,3},{1,0},{3,2},{4,5},{6,7},{5,4},{7,6},{8,9},{10,11},{9,8... | collective-permute-start | bytes 2519048 | tf_op jit(solution)/shard_map/ppermute | solution.py:509
  5.2 0.7 collective-permute-start.1
  5.9 1.5 %copy-done = bf16[641,1282]{1,0:T(8,128)(2,1)S(1)} copy-done((bf16[641,1282]{1,0:T(8,128)(2,1)S(1)}, bf16[641,1282]{1,0:T(8,128)(2,1)}, u32[]{:S(2)}) %copy-start) | copy-done | bytes 1643548
  7.4 0.9 copy-done.4
  8.3 0.9 copy-done.6
  9.2 0.9 copy-done.7
  10.1 0.7 copy-done.8
  10.8 0.7 copy-done.9
  11.5 1.4 %shard_map.127 = (f32[320,641]{1,0:T(8,128)S(1)}, f32[1,641]{1,0:T(1,128)S(1)}, f32[72,320]{1,0:T(8,128)S(1)}, f32[72,320]{1,0:T(8,128)S(1)}) custom-call(f32[2,160,641]{2,1,0:T(8,128)S(1)} %bitcast.13, f32[25,641]{1,0:T(8,128)S(1)} %copy-done.6, f32[641]{0:T(1024)S(1)} %copy-done.8, f32[72,2,160]{2,1,0:T(2,128)S(1)} %copy-done.7, f32[72]{0:T(128)S(1)} %copy-done.9, ...), custom_call_target="tpu_custom_call" | custom-call | flops 100000000 | bytes 3722784 | tf_op jit(solution)/shard_map/pallas_call | solution.py:124
  12.9 11.0 %collective-permute-done.first_ref = f32[328,640]{1,0:T(8,128)S(1)} collective-permute-done((f32[328,640]{1,0:T(8,128)S(1)}, f32[328,640]{1,0:T(8,128)S(1)}, u32[]{:S(2)}, u32[]{:S(2)}) %collective-permute-start) | collective-permute-done | bytes 839712 | tf_op jit(solution)/shard_map/ppermute | solution.py:509
  23.9 5.2 %shard_map.129 = (f32[72,320]{1,0:T(8,128)S(1)}, f32[72,320]{1,0:T(8,128)S(1)}, f32[6,176,641]{2,1,0:T(8,128)S(1)}, f32[320,641]{1,0:T(8,128)S(1)}, f32[320,1]{1...) custom-call(f32[2,160,641]{2,1,0:T(8,128)S(1)} %bitcast.14, ...), custom_call_target="tpu_custom_call" | custom-call | flops 1051855360 | bytes 14264320 | tf_op jit(solution)/shard_map/pallas_call | solution.py:124
  29.1 2.7 %collective-permute-start.2 = (f32[72,320]{1,0:T(8,128)S(1)}, f32[72,320]{1,0:T(8,128)S(1)}, u32[]{:S(2)}, u32[]{:S(2)}) collective-permute-start(f32[72,320]{1,0:T(8,128)S(1)} %get-tuple-element.54.refs_7_), channel_id=1, source_target_pairs={{0,24},{4,28},{8,16},{12,20},{16,8},{20,12},{24,0},{28,4},{1,25},{... | collective-permute-start | bytes 276488 | tf_op jit(solution)/shard_map/ppermute | solution.py:24
  31.8 0.5 collective-permute-start.3
  32.3 0.3 collective-permute-start.4
  32.7 2.9 %collective-permute-done.2.refs_0_ = f32[72,320]{1,0:T(8,128)S(1)} collective-permute-done((f32[72,320]{1,0:T(8,128)S(1)}, f32[72,320]{1,0:T(8,128)S(1)}, u32[]{:S(2)}, u32[]{:S(2)}) %collective-permute-start.2) | collective-permute-done | bytes 92192 | tf_op jit(solution)/shard_map/ppermute | solution.py:24
  35.6 1.0 collective-permute-done.3.refs_1_
  36.6 0.4 collective-permute-done.4.refs_2_
  37.2 0.8 collective-permute-done.7.refs_5_
  37.9 0.4 collective-permute-done.8.refs_6_
  38.4 2.5 %shard_map.130 = (f32[384,640]{1,0:T(8,128)S(1)}, f32[384,640]{1,0:T(8,128)S(1)}, f32[320,641]{1,0:T(8,128)S(1)}, bf16[320,1282]{1,0:T(8,128)(2,1)S(1)}, f32[72,...) custom-call(f32[72,320]{1,0:T(8,128)S(1)} %collective-permute-done.2.refs_0_, ...), custom_call_target="tpu_custom_call" | custom-call | flops 1051855360 | bytes 10120692 | tf_op jit(solution)/shard_map/pallas_call | solution.py:124
  40.9 0.3 collective-permute-start.9
  41.1 2.4 %collective-permute-done.9.refs_1_ = f32[384,640]{1,0:T(8,128)S(1)} collective-permute-done((f32[384,640]{1,0:T(8,128)S(1)}, f32[384,640]{1,0:T(8,128)S(1)}, u32[]{:S(2)}, u32[]{:S(2)}) %collective-permute-start.9) | collective-permute-done | bytes 983072 | tf_op jit(solution)/shard_map/ppermute | solution.py:24
  43.6 5.9 %shard_map.136 = (f32[384,640]{1,0:T(8,128)S(1)}, f32[384,640]{1,0:T(8,128)S(1)}) custom-call(bf16[320,1282]{1,0:T(8,128)(2,1)S(1)} %get-tuple-element.71.preact_ref, bf16[641,320]{1,0:T(8,128)(2,1)S(1)} %get-tuple-element.60.refs_15_.turned_ref, bf16[320,641]{1,0:T(8,128)(2,1)S(1)} %get-tuple-element.72.scaled_ref, bf16[641,1282]{1,0:T(8,128)(2,1)S(1)} %copy-done.1, ...), custom_call_target="tpu_custom_call" | custom-call | flops 1051855360 | bytes 10423016 | tf_op jit(solution)/shard_map/pallas_call | solution.py:124
  49.5 0.3 collective-permute-start.23
  49.8 1.9 %collective-permute-start.10 = (bf16[96,640]{1,0:T(8,128)(2,1)S(1)}, bf16[96,640]{1,0:T(8,128)(2,1)S(1)}, u32[]{:S(2)}, u32[]{:S(2)}) collective-permute-start(bf16[96,640]{1,0:T(8,128)(2,1)S(1)} %get-tuple-element.64), channel_id=1, source_target_pairs={{0,24},{4,28},{8,16},{12,20},{16,8},{20,12},{24,0},{28,4},{1,25},{... | collective-permute-start | bytes 368648 | tf_op jit(solution)/shard_map/ppermute | solution.py:24
  51.7 0.6 collective-permute-start.11
  52.3 1.0 collective-permute-start.12
  53.3 3.6 %collective-permute-done.10.refs_1_ = bf16[96,640]{1,0:T(8,128)(2,1)S(1)} collective-permute-done((bf16[96,640]{1,0:T(8,128)(2,1)S(1)}, bf16[96,640]{1,0:T(8,128)(2,1)S(1)}, u32[]{:S(2)}, u32[]{:S(2)}) %collective-permute-start.10) | collective-permute-done | bytes 122912 | tf_op jit(solution)/shard_map/ppermute | solution.py:24
  56.9 1.5 %collective-permute-done.11.refs_2_ = bf16[96,640]{1,0:T(8,128)(2,1)S(1)} collective-permute-done((bf16[96,640]{1,0:T(8,128)(2,1)S(1)}, bf16[96,640]{1,0:T(8,128)(2,1)S(1)}, u32[]{:S(2)}, u32[]{:S(2)}) %collective-permute-start.11) | collective-permute-done | bytes 122912 | tf_op jit(solution)/shard_map/ppermute | solution.py:24
  58.4 0.4 collective-permute-done.12.refs_3_
  59.0 3.7 %collective-permute-start.13 = (bf16[24,640]{1,0:T(8,128)(2,1)S(1)}, bf16[24,640]{1,0:T(8,128)(2,1)S(1)}, u32[]{:S(2)}, u32[]{:S(2)}) collective-permute-start(bf16[24,640]{1,0:T(8,128)(2,1)S(1)} %get-tuple-element.68), channel_id=1, source_target_pairs={{0,3},{1,2},{2,1},{3,0},{4,7},{5,6},{6,5},{7,4},{8,11},{9,10},{10,... | collective-permute-start | bytes 92168 | tf_op jit(solution)/shard_map/ppermute | solution.py:24
  62.6 2.7 %collective-permute-start.14 = (bf16[24,640]{1,0:T(8,128)(2,1)S(1)}, bf16[24,640]{1,0:T(8,128)(2,1)S(1)}, u32[]{:S(2)}, u32[]{:S(2)}) collective-permute-start(bf16[24,640]{1,0:T(8,128)(2,1)S(1)} %get-tuple-element.69), channel_id=1, source_target_pairs={{0,1},{1,0},{2,3},{3,2},{4,5},{5,4},{6,7},{7,6},{8,9},{9,8},{10,11... | collective-permute-start | bytes 92168 | tf_op jit(solution)/shard_map/ppermute | solution.py:24
  65.5 1.7 %collective-permute-start.24 = (bf16[96,640]{1,0:T(8,128)(2,1)S(1)}, bf16[96,640]{1,0:T(8,128)(2,1)S(1)}, u32[]{:S(2)}, u32[]{:S(2)}) collective-permute-start(bf16[96,640]{1,0:T(8,128)(2,1)S(1)} %get-tuple-element.83), channel_id=1, source_target_pairs={{0,24},{4,28},{8,16},{12,20},{16,8},{20,12},{24,0},{28,4},{1,25},{... | collective-permute-start | bytes 368648 | tf_op jit(solution)/shard_map/ppermute | solution.py:24
  67.2 0.6 collective-permute-start.25
  67.8 1.3 %collective-permute-start.26 = (bf16[96,640]{1,0:T(8,128)(2,1)S(1)}, bf16[96,640]{1,0:T(8,128)(2,1)S(1)}, u32[]{:S(2)}, u32[]{:S(2)}) collective-permute-start(bf16[96,640]{1,0:T(8,128)(2,1)S(1)} %get-tuple-element.85), channel_id=1, source_target_pairs={{0,16},{4,20},{8,24},{12,28},{16,0},{20,4},{24,8},{28,12},{1,17},{... | collective-permute-start | bytes 368648 | tf_op jit(solution)/shard_map/ppermute | solution.py:24
  69.1 1.1 collective-permute-done.15.refs_3_
  70.2 1.6 %collective-permute-start.16 = (bf16[24,640]{1,0:T(8,128)(2,1)S(1)}, bf16[24,640]{1,0:T(8,128)(2,1)S(1)}, u32[]{:S(2)}, u32[]{:S(2)}) collective-permute-start(bf16[24,640]{1,0:T(8,128)(2,1)S(1)} %shard_map.133.own_ref), channel_id=1, source_target_pairs={{0,3},{1,2},{2,1},{3,0},{4,7},{5,6},{6,5},{7,4},{8,11},{9,10},{10,... | collective-permute-start | bytes 92168 | tf_op jit(solution)/shard_map/ppermute | solution.py:24
  71.7 0.9 collective-permute-start.17
  72.7 3.5 %collective-permute-done.16.refs_0_ = bf16[24,640]{1,0:T(8,128)(2,1)S(1)} collective-permute-done((bf16[24,640]{1,0:T(8,128)(2,1)S(1)}, bf16[24,640]{1,0:T(8,128)(2,1)S(1)}, u32[]{:S(2)}, u32[]{:S(2)}) %collective-permute-start.16) | collective-permute-done | bytes 30752 | tf_op jit(solution)/shard_map/ppermute | solution.py:24
  76.2 4.8 %collective-permute-done.18.refs_2_ = bf16[24,640]{1,0:T(8,128)(2,1)S(1)} collective-permute-done((bf16[24,640]{1,0:T(8,128)(2,1)S(1)}, bf16[24,640]{1,0:T(8,128)(2,1)S(1)}, u32[]{:S(2)}, u32[]{:S(2)}) %collective-permute-start.18) | collective-permute-done | bytes 30752 | tf_op jit(solution)/shard_map/ppermute | solution.py:24
  81.1 1.6 %collective-permute-start.19 = (bf16[96,640]{1,0:T(8,128)(2,1)S(1)}, bf16[96,640]{1,0:T(8,128)(2,1)S(1)}, u32[]{:S(2)}, u32[]{:S(2)}) collective-permute-start(bf16[96,640]{1,0:T(8,128)(2,1)S(1)} %bitcast.24), channel_id=1, source_target_pairs={{0,24},{4,28},{8,16},{12,20},{16,8},{20,12},{24,0},{28,4},{1,25},{... | collective-permute-start | bytes 368648 | tf_op jit(solution)/shard_map/ppermute | solution.py:24
  82.8 1.5 %collective-permute-start.27 = (bf16[24,640]{1,0:T(8,128)(2,1)S(1)}, bf16[24,640]{1,0:T(8,128)(2,1)S(1)}, u32[]{:S(2)}, u32[]{:S(2)}) collective-permute-start(bf16[24,640]{1,0:T(8,128)(2,1)S(1)} %get-tuple-element.87), channel_id=1, source_target_pairs={{0,3},{1,2},{2,1},{3,0},{4,7},{5,6},{6,5},{7,4},{8,11},{9,10},{10,... | collective-permute-start | bytes 92168 | tf_op jit(solution)/shard_map/ppermute | solution.py:24
  84.3 2.9 %collective-permute-start.29 = (bf16[24,640]{1,0:T(8,128)(2,1)S(1)}, bf16[24,640]{1,0:T(8,128)(2,1)S(1)}, u32[]{:S(2)}, u32[]{:S(2)}) collective-permute-start(bf16[24,640]{1,0:T(8,128)(2,1)S(1)} %get-tuple-element.89), channel_id=1, source_target_pairs={{0,2},{1,3},{2,0},{3,1},{4,6},{5,7},{6,4},{7,5},{8,10},{9,11},{10,... | collective-permute-start | bytes 92168 | tf_op jit(solution)/shard_map/ppermute | solution.py:24
  87.2 1.5 %collective-permute-done.27.refs_1_ = bf16[24,640]{1,0:T(8,128)(2,1)S(1)} collective-permute-done((bf16[24,640]{1,0:T(8,128)(2,1)S(1)}, bf16[24,640]{1,0:T(8,128)(2,1)S(1)}, u32[]{:S(2)}, u32[]{:S(2)}) %collective-permute-start.27) | collective-permute-done | bytes 30752 | tf_op jit(solution)/shard_map/ppermute | solution.py:24
  88.7 0.8 collective-permute-done.28.refs_2_
  89.5 2.0 %collective-permute-start.30 = (bf16[24,640]{1,0:T(8,128)(2,1)S(1)}, bf16[24,640]{1,0:T(8,128)(2,1)S(1)}, u32[]{:S(2)}, u32[]{:S(2)}) collective-permute-start(bf16[24,640]{1,0:T(8,128)(2,1)S(1)} %shard_map.139.own_ref), channel_id=1, source_target_pairs={{0,3},{1,2},{2,1},{3,0},{4,7},{5,6},{6,5},{7,4},{8,11},{9,10},{10,... | collective-permute-start | bytes 92168 | tf_op jit(solution)/shard_map/ppermute | solution.py:24
  91.6 1.1 %collective-permute-start.31 = (bf16[24,640]{1,0:T(8,128)(2,1)S(1)}, bf16[24,640]{1,0:T(8,128)(2,1)S(1)}, u32[]{:S(2)}, u32[]{:S(2)}) collective-permute-start(bf16[24,640]{1,0:T(8,128)(2,1)S(1)} %shard_map.139.own_ref), channel_id=1, source_target_pairs={{0,1},{1,0},{2,3},{3,2},{4,5},{5,4},{6,7},{7,6},{8,9},{9,8},{10,11... | collective-permute-start | bytes 92168 | tf_op jit(solution)/shard_map/ppermute | solution.py:24
  92.7 1.3 %collective-permute-start.32 = (bf16[24,640]{1,0:T(8,128)(2,1)S(1)}, bf16[24,640]{1,0:T(8,128)(2,1)S(1)}, u32[]{:S(2)}, u32[]{:S(2)}) collective-permute-start(bf16[24,640]{1,0:T(8,128)(2,1)S(1)} %shard_map.139.own_ref), channel_id=1, source_target_pairs={{0,2},{1,3},{2,0},{3,1},{4,6},{5,7},{6,4},{7,5},{8,10},{9,11},{10,... | collective-permute-start | bytes 92168 | tf_op jit(solution)/shard_map/ppermute | solution.py:24
  94.0 0.3 collective-permute-start.20
  94.3 1.0 collective-permute-done.30.refs_0_
  95.3 1.0 collective-permute-start.21
  96.3 1.1 %collective-permute-done.32.refs_2_ = bf16[24,640]{1,0:T(8,128)(2,1)S(1)} collective-permute-done((bf16[24,640]{1,0:T(8,128)(2,1)S(1)}, bf16[24,640]{1,0:T(8,128)(2,1)S(1)}, u32[]{:S(2)}, u32[]{:S(2)}) %collective-permute-start.32) | collective-permute-done | bytes 30752 | tf_op jit(solution)/shard_map/ppermute | solution.py:24
  97.5 1.4 %collective-permute-start.33 = (bf16[96,640]{1,0:T(8,128)(2,1)S(1)}, bf16[96,640]{1,0:T(8,128)(2,1)S(1)}, u32[]{:S(2)}, u32[]{:S(2)}) collective-permute-start(bf16[96,640]{1,0:T(8,128)(2,1)S(1)} %bitcast.28), channel_id=1, source_target_pairs={{0,24},{4,28},{8,16},{12,20},{16,8},{20,12},{24,0},{28,4},{1,25},{... | collective-permute-start | bytes 368648 | tf_op jit(solution)/shard_map/ppermute | solution.py:24
  98.9 1.4 %collective-permute-start.34 = (bf16[96,640]{1,0:T(8,128)(2,1)S(1)}, bf16[96,640]{1,0:T(8,128)(2,1)S(1)}, u32[]{:S(2)}, u32[]{:S(2)}) collective-permute-start(bf16[96,640]{1,0:T(8,128)(2,1)S(1)} %bitcast.29), channel_id=1, source_target_pairs={{0,8},{4,12},{8,0},{12,4},{16,24},{20,28},{24,16},{28,20},{1,9},{5... | collective-permute-start | bytes 368648 | tf_op jit(solution)/shard_map/ppermute | solution.py:24
  100.4 0.7 collective-permute-start.35
  101.2 2.1 %collective-permute-done.33.refs_0_ = bf16[96,640]{1,0:T(8,128)(2,1)S(1)} collective-permute-done((bf16[96,640]{1,0:T(8,128)(2,1)S(1)}, bf16[96,640]{1,0:T(8,128)(2,1)S(1)}, u32[]{:S(2)}, u32[]{:S(2)}) %collective-permute-start.33) | collective-permute-done | bytes 122912 | tf_op jit(solution)/shard_map/ppermute | solution.py:24
  103.3 1.2 %collective-permute-done.34.refs_1_ = bf16[96,640]{1,0:T(8,128)(2,1)S(1)} collective-permute-done((bf16[96,640]{1,0:T(8,128)(2,1)S(1)}, bf16[96,640]{1,0:T(8,128)(2,1)S(1)}, u32[]{:S(2)}, u32[]{:S(2)}) %collective-permute-start.34) | collective-permute-done | bytes 122912 | tf_op jit(solution)/shard_map/ppermute | solution.py:24
  104.5 0.7 collective-permute-done.35.refs_2_
  105.4 0.2 copy.14.head_ref
  105.6 1.7 %collective-permute-done.36.got_two_ref = bf16[384,640]{1,0:T(8,128)(2,1)S(1)} collective-permute-done((bf16[384,640]{1,0:T(8,128)(2,1)S(1)}, bf16[384,640]{1,0:T(8,128)(2,1)S(1)}, u32[]{:S(2)}, u32[]{:S(2)}) %collective-permute-start.36) | collective-permute-done | bytes 491552 | tf_op jit(solution)/shard_map/ppermute | solution.py:24
  107.3 4.0 %shard_map.142 = (f32[1,1]{1,0:T(1,128)}, f32[25,641]{1,0:T(8,128)}, f32[1,641]{1,0:T(1,128)S(1)}, f32[641,1282]{1,0:T(8,128)}, f32[641,1282]{1,0:T(8,128)}, /*index=5*/f32[72,641]{1,0:T(8,128)}) custom-call(bf16[384,640]{1,0:T(8,128)(2,1)S(1)} %bitcast.18, bf16[384,640]{1,0:T(8,128)(2,1)S(1)} %collective-permute-done.22.got_one_ref, ...), custom_call_target="tpu_custom_call" | custom-call | flops 131481920 | bytes 8883756 | tf_op jit(solution)/shard_map/pallas_call | solution.py:124
  111.2 0.6 reduce
  (48 shorter events, 1.0 us)
Async XLA Ops:
  0.6 23.3 %copy-start.1 = (bf16[641,1282]{1,0:T(8,128)(2,1)S(1)}, bf16[641,1282]{1,0:T(8,128)(2,1)}, u32[]{:S(2)}) copy-start(bf16[641,1282]{1,0:T(8,128)(2,1)} %up_ref.3) | copy-start | bytes 4930576
  0.6 1.3 %copy-start.2 = (f32[1,641,2,160]{1,3,2,0:T(8,128)S(1)}, f32[1,641,2,160]{1,3,2,0:T(8,128)}, u32[]{:S(2)}) copy-start(f32[1,641,2,160]{1,3,2,0:T(8,128)} %param.8) | copy-start | bytes 2461444
  2.1 21.8 %collective-permute-start = (f32[328,640]{1,0:T(8,128)S(1)}, f32[328,640]{1,0:T(8,128)S(1)}, u32[]{:S(2)}, u32[]{:S(2)}) collective-permute-start(f32[328,640]{1,0:T(8,128)S(1)} %shard_map.128), channel_id=1, source_target_pairs={{0,1},{2,3},{1,0},{3,2},{4,5},{6,7},{5,4},{7,6},{8,9},{10,11},{9,8... | collective-permute-start | bytes 2519048 | tf_op jit(solution)/shard_map/ppermute | solution.py:509
  5.2 18.7 %collective-permute-start.1 = (f32[328,640]{1,0:T(8,128)S(1)}, f32[328,640]{1,0:T(8,128)S(1)}, u32[]{:S(2)}, u32[]{:S(2)}) collective-permute-start(f32[328,640]{1,0:T(8,128)S(1)} %shard_map.128), channel_id=1, source_target_pairs={{1,2},{2,1},{5,6},{6,5},{9,10},{10,9},{13,14},{14,13},{17,18},{18,... | collective-permute-start | bytes 2519048 | tf_op jit(solution)/shard_map/ppermute | solution.py:509
  5.9 1.5 %copy-start = (bf16[641,1282]{1,0:T(8,128)(2,1)S(1)}, bf16[641,1282]{1,0:T(8,128)(2,1)}, u32[]{:S(2)}) copy-start(bf16[641,1282]{1,0:T(8,128)(2,1)} %up_ref.3) | copy-start | bytes 4930576
  7.4 0.9 copy-start.4
  8.3 0.9 copy-start.6
  9.2 0.9 copy-start.7
  10.1 0.7 copy-start.8
  10.8 0.7 copy-start.9
  11.5 12.4 %copy-start.3 = (bf16[1282,641]{0,1:T(8,128)(2,1)S(1)}, bf16[1282,641]{0,1:T(8,128)(2,1)}, u32[]{:S(2)}) copy-start(bf16[1282,641]{0,1:T(8,128)(2,1)} %param.12) | copy-start | bytes 4930576
  11.5 12.4 %copy-start.5 = (bf16[641,72]{0,1:T(8,128)(2,1)S(1)}, bf16[641,72]{0,1:T(8,128)(2,1)}, u32[]{:S(2)}) copy-start(bf16[641,72]{0,1:T(8,128)(2,1)} %param.13) | copy-start | bytes 276916
  29.1 6.5 %collective-permute-start.2 = (f32[72,320]{1,0:T(8,128)S(1)}, f32[72,320]{1,0:T(8,128)S(1)}, u32[]{:S(2)}, u32[]{:S(2)}) collective-permute-start(f32[72,320]{1,0:T(8,128)S(1)} %get-tuple-element.54.refs_7_), channel_id=1, source_target_pairs={{0,24},{4,28},{8,16},{12,20},{16,8},{20,12},{24,0},{28,4},{1,25},{... | collective-permute-start | bytes 276488 | tf_op jit(solution)/shard_map/ppermute | solution.py:24
  31.8 4.8 %collective-permute-start.3 = (f32[72,320]{1,0:T(8,128)S(1)}, f32[72,320]{1,0:T(8,128)S(1)}, u32[]{:S(2)}, u32[]{:S(2)}) collective-permute-start(f32[72,320]{1,0:T(8,128)S(1)} %get-tuple-element.54.refs_7_), channel_id=1, source_target_pairs={{0,8},{4,12},{8,0},{12,4},{16,24},{20,28},{24,16},{28,20},{1,9},{5... | collective-permute-start | bytes 276488 | tf_op jit(solution)/shard_map/ppermute | solution.py:24
  32.3 4.7 %collective-permute-start.4 = (f32[72,320]{1,0:T(8,128)S(1)}, f32[72,320]{1,0:T(8,128)S(1)}, u32[]{:S(2)}, u32[]{:S(2)}) collective-permute-start(f32[72,320]{1,0:T(8,128)S(1)} %get-tuple-element.54.refs_7_), channel_id=1, source_target_pairs={{0,16},{4,20},{8,24},{12,28},{16,0},{20,4},{24,8},{28,12},{1,17},{... | collective-permute-start | bytes 276488 | tf_op jit(solution)/shard_map/ppermute | solution.py:24
  32.7 4.5 %collective-permute-start.5 = (f32[72,320]{1,0:T(8,128)S(1)}, f32[72,320]{1,0:T(8,128)S(1)}, u32[]{:S(2)}, u32[]{:S(2)}) collective-permute-start(f32[72,320]{1,0:T(8,128)S(1)} %get-tuple-element.54.refs_7_), channel_id=1, source_target_pairs={{0,4},{4,0},{8,12},{12,8},{16,20},{20,16},{24,28},{28,24},{1,5},{5... | collective-permute-start | bytes 276488 | tf_op jit(solution)/shard_map/ppermute | solution.py:24
  35.6 1.6 %collective-permute-start.6 = (f32[72,320]{1,0:T(8,128)S(1)}, f32[72,320]{1,0:T(8,128)S(1)}, u32[]{:S(2)}, u32[]{:S(2)}) collective-permute-start(f32[72,320]{1,0:T(8,128)S(1)} %collective-permute-done.2.refs_0_), channel_id=1, source_target_pairs={{0,4},{4,0},{8,12},{12,8},{16,20},{20,16},{24,28},{28,24},{1,5},{5... | collective-permute-start | bytes 276488 | tf_op jit(solution)/shard_map/ppermute | solution.py:24
  36.6 1.3 %collective-permute-start.7 = (f32[72,320]{1,0:T(8,128)S(1)}, f32[72,320]{1,0:T(8,128)S(1)}, u32[]{:S(2)}, u32[]{:S(2)}) collective-permute-start(f32[72,320]{1,0:T(8,128)S(1)} %collective-permute-done.3.refs_1_), channel_id=1, source_target_pairs={{0,4},{4,0},{8,12},{12,8},{16,20},{20,16},{24,28},{28,24},{1,5},{5... | collective-permute-start | bytes 276488 | tf_op jit(solution)/shard_map/ppermute | solution.py:24
  37.1 1.3 %collective-permute-start.8 = (f32[72,320]{1,0:T(8,128)S(1)}, f32[72,320]{1,0:T(8,128)S(1)}, u32[]{:S(2)}, u32[]{:S(2)}) collective-permute-start(f32[72,320]{1,0:T(8,128)S(1)} %collective-permute-done.4.refs_2_), channel_id=1, source_target_pairs={{0,4},{4,0},{8,12},{12,8},{16,20},{20,16},{24,28},{28,24},{1,5},{5... | collective-permute-start | bytes 276488 | tf_op jit(solution)/shard_map/ppermute | solution.py:24
  40.9 2.6 %collective-permute-start.9 = (f32[384,640]{1,0:T(8,128)S(1)}, f32[384,640]{1,0:T(8,128)S(1)}, u32[]{:S(2)}, u32[]{:S(2)}) collective-permute-start(f32[384,640]{1,0:T(8,128)S(1)} %get-tuple-element.62), channel_id=1, source_target_pairs={{0,4},{4,0},{8,12},{12,8},{16,20},{20,16},{24,28},{28,24},{1,5},{5... | collective-permute-start | bytes 2949128 | tf_op jit(solution)/shard_map/ppermute | solution.py:24
  49.5 15.8 %collective-permute-start.23 = (f32[384,640]{1,0:T(8,128)S(1)}, f32[384,640]{1,0:T(8,128)S(1)}, u32[]{:S(2)}, u32[]{:S(2)}) collective-permute-start(f32[384,640]{1,0:T(8,128)S(1)} %get-tuple-element.81), channel_id=1, source_target_pairs={{0,4},{4,0},{8,12},{12,8},{16,20},{20,16},{24,28},{28,24},{1,5},{5... | collective-permute-start | bytes 2949128 | tf_op jit(solution)/shard_map/ppermute | solution.py:24
  49.8 7.1 %collective-permute-start.10 = (bf16[96,640]{1,0:T(8,128)(2,1)S(1)}, bf16[96,640]{1,0:T(8,128)(2,1)S(1)}, u32[]{:S(2)}, u32[]{:S(2)}) collective-permute-start(bf16[96,640]{1,0:T(8,128)(2,1)S(1)} %get-tuple-element.64), channel_id=1, source_target_pairs={{0,24},{4,28},{8,16},{12,20},{16,8},{20,12},{24,0},{28,4},{1,25},{... | collective-permute-start | bytes 368648 | tf_op jit(solution)/shard_map/ppermute | solution.py:24
  51.7 6.7 %collective-permute-start.11 = (bf16[96,640]{1,0:T(8,128)(2,1)S(1)}, bf16[96,640]{1,0:T(8,128)(2,1)S(1)}, u32[]{:S(2)}, u32[]{:S(2)}) collective-permute-start(bf16[96,640]{1,0:T(8,128)(2,1)S(1)} %get-tuple-element.65), channel_id=1, source_target_pairs={{0,8},{4,12},{8,0},{12,4},{16,24},{20,28},{24,16},{28,20},{1,9},{5... | collective-permute-start | bytes 368648 | tf_op jit(solution)/shard_map/ppermute | solution.py:24
  52.3 6.6 %collective-permute-start.12 = (bf16[96,640]{1,0:T(8,128)(2,1)S(1)}, bf16[96,640]{1,0:T(8,128)(2,1)S(1)}, u32[]{:S(2)}, u32[]{:S(2)}) collective-permute-start(bf16[96,640]{1,0:T(8,128)(2,1)S(1)} %get-tuple-element.66), channel_id=1, source_target_pairs={{0,16},{4,20},{8,24},{12,28},{16,0},{20,4},{24,8},{28,12},{1,17},{... | collective-permute-start | bytes 368648 | tf_op jit(solution)/shard_map/ppermute | solution.py:24
  59.0 8.8 %collective-permute-start.13 = (bf16[24,640]{1,0:T(8,128)(2,1)S(1)}, bf16[24,640]{1,0:T(8,128)(2,1)S(1)}, u32[]{:S(2)}, u32[]{:S(2)}) collective-permute-start(bf16[24,640]{1,0:T(8,128)(2,1)S(1)} %get-tuple-element.68), channel_id=1, source_target_pairs={{0,3},{1,2},{2,1},{3,0},{4,7},{5,6},{6,5},{7,4},{8,11},{9,10},{10,... | collective-permute-start | bytes 92168 | tf_op jit(solution)/shard_map/ppermute | solution.py:24
  62.6 6.4 %collective-permute-start.14 = (bf16[24,640]{1,0:T(8,128)(2,1)S(1)}, bf16[24,640]{1,0:T(8,128)(2,1)S(1)}, u32[]{:S(2)}, u32[]{:S(2)}) collective-permute-start(bf16[24,640]{1,0:T(8,128)(2,1)S(1)} %get-tuple-element.69), channel_id=1, source_target_pairs={{0,1},{1,0},{2,3},{3,2},{4,5},{5,4},{6,7},{7,6},{8,9},{9,8},{10,11... | collective-permute-start | bytes 92168 | tf_op jit(solution)/shard_map/ppermute | solution.py:24
  65.4 4.8 %collective-permute-start.15 = (bf16[24,640]{1,0:T(8,128)(2,1)S(1)}, bf16[24,640]{1,0:T(8,128)(2,1)S(1)}, u32[]{:S(2)}, u32[]{:S(2)}) collective-permute-start(bf16[24,640]{1,0:T(8,128)(2,1)S(1)} %get-tuple-element.70), channel_id=1, source_target_pairs={{0,2},{1,3},{2,0},{3,1},{4,6},{5,7},{6,4},{7,5},{8,10},{9,11},{10,... | collective-permute-start | bytes 92168 | tf_op jit(solution)/shard_map/ppermute | solution.py:24
  65.5 17.2 %collective-permute-start.24 = (bf16[96,640]{1,0:T(8,128)(2,1)S(1)}, bf16[96,640]{1,0:T(8,128)(2,1)S(1)}, u32[]{:S(2)}, u32[]{:S(2)}) collective-permute-start(bf16[96,640]{1,0:T(8,128)(2,1)S(1)} %get-tuple-element.83), channel_id=1, source_target_pairs={{0,24},{4,28},{8,16},{12,20},{16,8},{20,12},{24,0},{28,4},{1,25},{... | collective-permute-start | bytes 368648 | tf_op jit(solution)/shard_map/ppermute | solution.py:24
  67.2 15.4 %collective-permute-start.25 = (bf16[96,640]{1,0:T(8,128)(2,1)S(1)}, bf16[96,640]{1,0:T(8,128)(2,1)S(1)}, u32[]{:S(2)}, u32[]{:S(2)}) collective-permute-start(bf16[96,640]{1,0:T(8,128)(2,1)S(1)} %get-tuple-element.84), channel_id=1, source_target_pairs={{0,8},{4,12},{8,0},{12,4},{16,24},{20,28},{24,16},{28,20},{1,9},{5... | collective-permute-start | bytes 368648 | tf_op jit(solution)/shard_map/ppermute | solution.py:24
  67.8 14.9 %collective-permute-start.26 = (bf16[96,640]{1,0:T(8,128)(2,1)S(1)}, bf16[96,640]{1,0:T(8,128)(2,1)S(1)}, u32[]{:S(2)}, u32[]{:S(2)}) collective-permute-start(bf16[96,640]{1,0:T(8,128)(2,1)S(1)} %get-tuple-element.85), channel_id=1, source_target_pairs={{0,16},{4,20},{8,24},{12,28},{16,0},{20,4},{24,8},{28,12},{1,17},{... | collective-permute-start | bytes 368648 | tf_op jit(solution)/shard_map/ppermute | solution.py:24
  70.2 6.0 %collective-permute-start.16 = (bf16[24,640]{1,0:T(8,128)(2,1)S(1)}, bf16[24,640]{1,0:T(8,128)(2,1)S(1)}, u32[]{:S(2)}, u32[]{:S(2)}) collective-permute-start(bf16[24,640]{1,0:T(8,128)(2,1)S(1)} %shard_map.133.own_ref), channel_id=1, source_target_pairs={{0,3},{1,2},{2,1},{3,0},{4,7},{5,6},{6,5},{7,4},{8,11},{9,10},{10,... | collective-permute-start | bytes 92168 | tf_op jit(solution)/shard_map/ppermute | solution.py:24
  71.7 4.5 %collective-permute-start.17 = (bf16[24,640]{1,0:T(8,128)(2,1)S(1)}, bf16[24,640]{1,0:T(8,128)(2,1)S(1)}, u32[]{:S(2)}, u32[]{:S(2)}) collective-permute-start(bf16[24,640]{1,0:T(8,128)(2,1)S(1)} %shard_map.133.own_ref), channel_id=1, source_target_pairs={{0,1},{1,0},{2,3},{3,2},{4,5},{5,4},{6,7},{7,6},{8,9},{9,8},{10,11... | collective-permute-start | bytes 92168 | tf_op jit(solution)/shard_map/ppermute | solution.py:24
  76.2 4.8 %collective-permute-start.18 = (bf16[24,640]{1,0:T(8,128)(2,1)S(1)}, bf16[24,640]{1,0:T(8,128)(2,1)S(1)}, u32[]{:S(2)}, u32[]{:S(2)}) collective-permute-start(bf16[24,640]{1,0:T(8,128)(2,1)S(1)} %shard_map.133.own_ref), channel_id=1, source_target_pairs={{0,2},{1,3},{2,0},{3,1},{4,6},{5,7},{6,4},{7,5},{8,10},{9,11},{10,... | collective-permute-start | bytes 92168 | tf_op jit(solution)/shard_map/ppermute | solution.py:24
  81.1 19.3 %collective-permute-start.19 = (bf16[96,640]{1,0:T(8,128)(2,1)S(1)}, bf16[96,640]{1,0:T(8,128)(2,1)S(1)}, u32[]{:S(2)}, u32[]{:S(2)}) collective-permute-start(bf16[96,640]{1,0:T(8,128)(2,1)S(1)} %bitcast.24), channel_id=1, source_target_pairs={{0,24},{4,28},{8,16},{12,20},{16,8},{20,12},{24,0},{28,4},{1,25},{... | collective-permute-start | bytes 368648 | tf_op jit(solution)/shard_map/ppermute | solution.py:24
  82.8 5.9 %collective-permute-start.27 = (bf16[24,640]{1,0:T(8,128)(2,1)S(1)}, bf16[24,640]{1,0:T(8,128)(2,1)S(1)}, u32[]{:S(2)}, u32[]{:S(2)}) collective-permute-start(bf16[24,640]{1,0:T(8,128)(2,1)S(1)} %get-tuple-element.87), channel_id=1, source_target_pairs={{0,3},{1,2},{2,1},{3,0},{4,7},{5,6},{6,5},{7,4},{8,11},{9,10},{10,... | collective-permute-start | bytes 92168 | tf_op jit(solution)/shard_map/ppermute | solution.py:24
  84.3 5.2 %collective-permute-start.28 = (bf16[24,640]{1,0:T(8,128)(2,1)S(1)}, bf16[24,640]{1,0:T(8,128)(2,1)S(1)}, u32[]{:S(2)}, u32[]{:S(2)}) collective-permute-start(bf16[24,640]{1,0:T(8,128)(2,1)S(1)} %get-tuple-element.88), channel_id=1, source_target_pairs={{0,1},{1,0},{2,3},{3,2},{4,5},{5,4},{6,7},{7,6},{8,9},{9,8},{10,11... | collective-permute-start | bytes 92168 | tf_op jit(solution)/shard_map/ppermute | solution.py:24
  84.3 5.2 %collective-permute-start.29 = (bf16[24,640]{1,0:T(8,128)(2,1)S(1)}, bf16[24,640]{1,0:T(8,128)(2,1)S(1)}, u32[]{:S(2)}, u32[]{:S(2)}) collective-permute-start(bf16[24,640]{1,0:T(8,128)(2,1)S(1)} %get-tuple-element.89), channel_id=1, source_target_pairs={{0,2},{1,3},{2,0},{3,1},{4,6},{5,7},{6,4},{7,5},{8,10},{9,11},{10,... | collective-permute-start | bytes 92168 | tf_op jit(solution)/shard_map/ppermute | solution.py:24
  89.5 5.8 %collective-permute-start.30 = (bf16[24,640]{1,0:T(8,128)(2,1)S(1)}, bf16[24,640]{1,0:T(8,128)(2,1)S(1)}, u32[]{:S(2)}, u32[]{:S(2)}) collective-permute-start(bf16[24,640]{1,0:T(8,128)(2,1)S(1)} %shard_map.139.own_ref), channel_id=1, source_target_pairs={{0,3},{1,2},{2,1},{3,0},{4,7},{5,6},{6,5},{7,4},{8,11},{9,10},{10,... | collective-permute-start | bytes 92168 | tf_op jit(solution)/shard_map/ppermute | solution.py:24
  91.6 4.8 %collective-permute-start.31 = (bf16[24,640]{1,0:T(8,128)(2,1)S(1)}, bf16[24,640]{1,0:T(8,128)(2,1)S(1)}, u32[]{:S(2)}, u32[]{:S(2)}) collective-permute-start(bf16[24,640]{1,0:T(8,128)(2,1)S(1)} %shard_map.139.own_ref), channel_id=1, source_target_pairs={{0,1},{1,0},{2,3},{3,2},{4,5},{5,4},{6,7},{7,6},{8,9},{9,8},{10,11... | collective-permute-start | bytes 92168 | tf_op jit(solution)/shard_map/ppermute | solution.py:24
  92.7 4.8 %collective-permute-start.32 = (bf16[24,640]{1,0:T(8,128)(2,1)S(1)}, bf16[24,640]{1,0:T(8,128)(2,1)S(1)}, u32[]{:S(2)}, u32[]{:S(2)}) collective-permute-start(bf16[24,640]{1,0:T(8,128)(2,1)S(1)} %shard_map.139.own_ref), channel_id=1, source_target_pairs={{0,2},{1,3},{2,0},{3,1},{4,6},{5,7},{6,4},{7,5},{8,10},{9,11},{10,... | collective-permute-start | bytes 92168 | tf_op jit(solution)/shard_map/ppermute | solution.py:24
  94.0 7.1 %collective-permute-start.20 = (bf16[96,640]{1,0:T(8,128)(2,1)S(1)}, bf16[96,640]{1,0:T(8,128)(2,1)S(1)}, u32[]{:S(2)}, u32[]{:S(2)}) collective-permute-start(bf16[96,640]{1,0:T(8,128)(2,1)S(1)} %bitcast.25), channel_id=1, source_target_pairs={{0,8},{4,12},{8,0},{12,4},{16,24},{20,28},{24,16},{28,20},{1,9},{5... | collective-permute-start | bytes 368648 | tf_op jit(solution)/shard_map/ppermute | solution.py:24
  95.3 5.8 %collective-permute-start.21 = (bf16[96,640]{1,0:T(8,128)(2,1)S(1)}, bf16[96,640]{1,0:T(8,128)(2,1)S(1)}, u32[]{:S(2)}, u32[]{:S(2)}) collective-permute-start(bf16[96,640]{1,0:T(8,128)(2,1)S(1)} %bitcast.26), channel_id=1, source_target_pairs={{0,16},{4,20},{8,24},{12,28},{16,0},{20,4},{24,8},{28,12},{1,17},{... | collective-permute-start | bytes 368648 | tf_op jit(solution)/shard_map/ppermute | solution.py:24
  97.5 5.8 %collective-permute-start.33 = (bf16[96,640]{1,0:T(8,128)(2,1)S(1)}, bf16[96,640]{1,0:T(8,128)(2,1)S(1)}, u32[]{:S(2)}, u32[]{:S(2)}) collective-permute-start(bf16[96,640]{1,0:T(8,128)(2,1)S(1)} %bitcast.28), channel_id=1, source_target_pairs={{0,24},{4,28},{8,16},{12,20},{16,8},{20,12},{24,0},{28,4},{1,25},{... | collective-permute-start | bytes 368648 | tf_op jit(solution)/shard_map/ppermute | solution.py:24
  98.9 5.6 %collective-permute-start.34 = (bf16[96,640]{1,0:T(8,128)(2,1)S(1)}, bf16[96,640]{1,0:T(8,128)(2,1)S(1)}, u32[]{:S(2)}, u32[]{:S(2)}) collective-permute-start(bf16[96,640]{1,0:T(8,128)(2,1)S(1)} %bitcast.29), channel_id=1, source_target_pairs={{0,8},{4,12},{8,0},{12,4},{16,24},{20,28},{24,16},{28,20},{1,9},{5... | collective-permute-start | bytes 368648 | tf_op jit(solution)/shard_map/ppermute | solution.py:24
  100.4 4.9 %collective-permute-start.35 = (bf16[96,640]{1,0:T(8,128)(2,1)S(1)}, bf16[96,640]{1,0:T(8,128)(2,1)S(1)}, u32[]{:S(2)}, u32[]{:S(2)}) collective-permute-start(bf16[96,640]{1,0:T(8,128)(2,1)S(1)} %bitcast.30), channel_id=1, source_target_pairs={{0,16},{4,20},{8,24},{12,28},{16,0},{20,4},{24,8},{28,12},{1,17},{... | collective-permute-start | bytes 368648 | tf_op jit(solution)/shard_map/ppermute | solution.py:24
  101.1 4.4 %collective-permute-start.22 = (bf16[384,640]{1,0:T(8,128)(2,1)S(1)}, bf16[384,640]{1,0:T(8,128)(2,1)S(1)}, u32[]{:S(2)}, u32[]{:S(2)}) collective-permute-start(bf16[384,640]{1,0:T(8,128)(2,1)S(1)} %bitcast.17), channel_id=1, source_target_pairs={{0,4},{4,0},{8,12},{12,8},{16,20},{20,16},{24,28},{28,24},{1,5},{5... | collective-permute-start | bytes 1474568 | tf_op jit(solution)/shard_map/ppermute | solution.py:24
  105.3 1.9 %collective-permute-start.36 = (bf16[384,640]{1,0:T(8,128)(2,1)S(1)}, bf16[384,640]{1,0:T(8,128)(2,1)S(1)}, u32[]{:S(2)}, u32[]{:S(2)}) collective-permute-start(bf16[384,640]{1,0:T(8,128)(2,1)S(1)} %bitcast.19), channel_id=1, source_target_pairs={{0,4},{4,0},{8,12},{12,8},{16,20},{20,16},{24,28},{28,24},{1,5},{5... | collective-permute-start | bytes 1474568 | tf_op jit(solution)/shard_map/ppermute | solution.py:24
where the time goes:
time: 112 us
  waiting for transfers between devices  44.2 us (39%)
  starting transfers between devices  39.4 us (35%)
  Pallas kernels  19.7 us (18%)
  local copies, waits for them, and re-layouts  7.03 us (6%)
    ppermute x35, starting transfers between devices, swap(): return lax.ppermute(value, axis, [(i, i ^ mask) for i in range(count)])  35.6 us
    ppermute x35, waiting for transfers between devices, swap(): return lax.ppermute(value, axis, [(i, i ^ mask) for i in range(count)])  33.2 us
    pallas_call x16, Pallas kernels, call(): pl.pallas_call(kernel, out_shape=outs, in_specs=[spec] * len(args), out_s...  19.7 us
    ppermute x2, waiting for transfers between devices, trade(): return lax.ppermute(value, 'lat', pairs + [(j, i) for i, j in pairs])  11 us
    unnamed x21, local copies, waits for them, and re-layouts  7.03 us
    ppermute x2, starting transfers between devices, trade(): return lax.ppermute(value, 'lat', pairs + [(j, i) for i, j in pairs])  3.78 us
  transfers between devices with their start and end apart: 37, of which 21 were waited for; matrix products, arithmetic and copies ran while one was open for 0% of the time, Pallas kernels for 2%

commit v1 on v0

--- a/solution.py
+++ b/solution.py
@@ -12,6 +12,7 @@
 DELTA = 0.1
 EPSILON = 1e-05
 BF = jnp.bfloat16
+EXTRA = (224, 32)
 F32 = jnp.float32
 
 
@@ -223,8 +224,8 @@
 
 def forward_kernel(
     field_ref, part_ref, first_ref, second_ref, kernel_ref, gain_ref, up_ref, down_ref, head_ref,
-    truth_ref, forecast_ref, miss_ref, win_ref, normed_ref, inverse_ref, scaled_ref, turned_ref, hidden_ref,
-    slope_ref, rounded_ref, summed_ref,
+    truth_ref, forecast_ref, miss_ref, win_ref, normed_ref, inverse_ref, scaled_ref, hidden_ref,
+    preact_ref, rounded_ref, summed_ref,
 ):
     height, width, channels = field_ref.shape
     lanes = first_ref.shape[1]
@@ -255,14 +256,12 @@
         inverse_ref[rows, :] = inverse
         scaled_ref[rows, :] = (normed * gain_ref[...]).astype(BF)
 
-    turned_ref[...] = scaled_ref[...].T
     for lo, hi in spans(up_ref.shape[1], 256):
         preact = dot(scaled_ref[...], up_ref[:, lo:hi], ((1,), (0,)))
+        preact_ref[:, lo:hi] = preact
         cumul = 0.5 * (1.0 + lax.erf(preact * (1.0 / math.sqrt(2.0))))
-        density = jnp.exp(-0.5 * preact * preact) * (1.0 / math.sqrt(2.0 * math.pi))
         hidden = (preact * cumul).astype(BF)
         hidden_ref[:, lo:hi] = hidden
-        slope_ref[:, lo:hi] = cumul + preact * density
         summed_ref[...] += dot(hidden, down_ref[:, lo:hi], ((1,), (1,)))
     rounded = summed_ref[...].astype(BF)
     rounded_ref[...] = rounded
@@ -271,12 +270,21 @@
     miss_ref[...] = forecast - truth_ref[...]
 
 
+def slope_kernel(preact_ref, scaled_ref, slope_ref, turned_ref):
+    turned_ref[...] = scaled_ref[...].T
+    for lo, hi in spans(preact_ref.shape[1], 256):
+        preact = preact_ref[:, lo:hi]
+        cumul = 0.5 * (1.0 + lax.erf(preact * (1.0 / math.sqrt(2.0))))
+        density = jnp.exp(-0.5 * preact * preact) * (1.0 / math.sqrt(2.0 * math.pi))
+        slope_ref[:, lo:hi] = cumul + preact * density
+
+
 def score_kernel(members, bands, count, *refs):
     other_refs = refs[: members - 1]
     (
         forecast_ref, miss_ref, weight_ref, head_ref, down_ref, rounded_ref, hidden_ref, slope_ref,
-        turned_ref, own_ref, sent_ref, output_ref, preact_ref, head_term_ref, factor_ref, loss_ref,
-        cot_ref, main_ref,
+        turned_ref, own_ref, sent_ref, output_ref, preact_ref,
+        cot_ref, main_ref, factor_ref, heads_ref,
     ) = refs[members - 1 :]
     fields, cells = forecast_ref.shape
     lanes = own_ref.shape[1]
@@ -301,10 +309,8 @@
     first = part.astype(BF).astype(F32)
     second = (part - first).astype(BF).astype(F32)
     third = part - first - second
-    slot = lax.broadcasted_iota(jnp.int32, (8, lanes), 1) == mine
-    line = lax.broadcasted_iota(jnp.int32, (8, lanes), 0)
-    value = jnp.where(line == 0, first, jnp.where(line == 1, second, third))
-    loss_ref[...] = jnp.where(slot & (line < 3), value, 0.0)
+    slot = lax.broadcasted_iota(jnp.int32, (1, lanes), 1) == mine
+    losses = [jnp.where(slot, value, 0.0) for value in (first, second, third)]
     cot = (
         weights
         * (miss * inverse - pair_der * (1.0 / (members - 1)))
@@ -314,7 +320,7 @@
     cot_ref[...] = jnp.zeros_like(cot_ref)
     cot_ref[:fields, :cells] = co.astype(F32)
     turned = cot_ref[...].T[:cells, :fields].astype(BF)
-    head_term_ref[...] = dot(co, rounded_ref[...], ((1,), (0,)))
+    head_term = dot(co, rounded_ref[...], ((1,), (0,)))
     d_output = dot(turned, head_ref[...], ((1,), (0,)))
     output_ref[...] = d_output
     d_round = d_output.astype(BF)
@@ -322,7 +328,26 @@
         factor_ref[:, lo:hi] = dot(co, hidden_ref[:, lo:hi], ((1,), (0,)))
         d_hidden = dot(d_round, down_ref[:, lo:hi], ((1,), (0,)))
         preact_ref[:, lo:hi] = (d_hidden * slope_ref[:, lo:hi]).astype(BF)
-    gradient_rows(main_ref, 0, main_ref.shape[0] * main_ref.shape[1], turned_ref, preact_ref)
+    size, piece, lanes = main_ref.shape
+    gradient_rows(main_ref, 0, size * piece - EXTRA[0], turned_ref, preact_ref)
+    out_ref = main_ref.at[size - 1]
+    halves = down_ref.shape[1] // lanes
+    even = halves * lanes
+    left = down_ref.shape[1] - even
+    at = piece - EXTRA[0]
+    for h in range(halves):
+        out_ref[at : at + fields, :] = factor_ref[:, h * lanes : (h + 1) * lanes]
+        at += fields
+    out_ref[at : at + fields, :] = head_term[:, :lanes]
+    at += fields
+    out_ref[at:, :] = jnp.zeros((piece - at, lanes), F32)
+    heads_ref[...] = jnp.zeros_like(heads_ref)
+    heads_ref[:fields, :left] = factor_ref[:, even:]
+    heads_ref[:fields, left : left + 1] = head_term[:, lanes:]
+    out_ref[at : at + left + 1, :128] = heads_ref[...].T[: left + 1]
+    at += left + 1
+    for n, value in enumerate(losses):
+        out_ref[at + n : at + n + 1, :] = value
     hand_out(stages()[0], main_ref, own_ref, [sent_ref])
 
 
@@ -339,56 +364,58 @@
         done += take
 
 
+def input_kernel(
+    preact_ref, up_ref, gain_ref, normed_ref, inverse_ref, output_ref, wide_ref, gain_row_ref
+):
+    channels = normed_ref.shape[1]
+    d_scaled = dot(preact_ref[...], up_ref[...], ((1,), (1,)))
+    normed = normed_ref[...]
+    gain_row_ref[...] = jnp.sum(d_scaled * normed, axis=0, keepdims=True)
+    d_normed = d_scaled * gain_ref[...]
+    d_summed = output_ref[...] + inverse_ref[...] * (
+        d_normed
+        - jnp.sum(d_normed, axis=1, keepdims=True) * (1.0 / channels)
+        - normed * (jnp.sum(d_normed * normed, axis=1, keepdims=True) * (1.0 / channels))
+    )
+    wide_ref[...] = d_summed
+
+
 def rest_kernel(
-    preact_ref, turned_ref, scaled_ref, up_ref, gain_ref, normed_ref, inverse_ref, output_ref,
-    win_ref, head_term_ref, factor_ref, loss_ref, after_ref,
-    own_ref, sent_ref, wide_ref, grads_ref, heads_ref, pieces_ref,
+    preact_ref, turned_ref, scaled_ref, win_ref, wide_ref, gain_row_ref, after_ref,
+    own_ref, sent_ref, grads_ref, pieces_ref,
 ):
-    cells, channels = normed_ref.shape
+    cells, channels = wide_ref.shape
     hidden_units = preact_ref.shape[1]
-    fields = head_term_ref.shape[0]
     size, piece, lanes = pieces_ref.shape
     halves = hidden_units // lanes
     even = halves * lanes
     height = win_ref.shape[0] - 4
     width = cells // height
-    base = size * piece - 256
-    gradient_rows(pieces_ref, halves * lanes - base, base, turned_ref, preact_ref)
+    base = size * piece - EXTRA[1]
+    gradient_rows(pieces_ref, even - base, base, turned_ref, preact_ref)
     out_ref = pieces_ref.at[size - 1]
-    base -= (size - 1) * piece
-    for h in range(halves):
-        at = base + h * fields
-        out_ref[at : at + fields, :] = factor_ref[:, h * lanes : (h + 1) * lanes]
-    at = base + halves * fields
-    out_ref[at : at + fields, :] = head_term_ref[:, :lanes]
-    at += fields
-
-    d_scaled = dot(preact_ref[...], up_ref[...], ((1,), (1,)))
-    normed = normed_ref[...]
+    at = piece - EXTRA[1]
+
     grads_ref[...] = jnp.zeros_like(grads_ref)
-    grads_ref[25:26, :channels] = jnp.sum(d_scaled * normed, axis=0, keepdims=True)
-    d_normed = d_scaled * gain_ref[...]
-    d_summed = output_ref[...] + inverse_ref[...] * (
-        d_normed
-        - jnp.sum(d_normed, axis=1, keepdims=True) * (1.0 / channels)
-        - normed * (jnp.sum(d_normed * normed, axis=1, keepdims=True) * (1.0 / channels))
-    )
-    wide_ref[...] = d_summed
+    grads_ref[25:26, :channels] = gain_row_ref[...]
+    part = width // 4
 
     def correlate(columns):
-        for a in range(5):
-            for b in range(5):
-                total = None
-                for i in range(height):
-                    term = jnp.sum(
-                        wide_ref[i * width : (i + 1) * width, columns]
-                        * win_ref[i + a, 6 + b : 6 + b + width, columns],
-                        axis=0,
-                        keepdims=True,
-                    )
-                    total = term if total is None else total + term
-                t = 5 * a + b
-                grads_ref[t : t + 1, columns] = total
+        acc = [None] * 25
+        for c in range(0, width, part):
+            d = [wide_ref[i * width + c : i * width + c + part, columns] for i in range(height)]
+            for w in range(height + 4):
+                for b in range(5):
+                    moved = win_ref[w, 6 + b + c : 6 + b + c + part, columns]
+                    for i in range(height):
+                        if 0 <= w - i < 5:
+                            t = 5 * (w - i) + b
+                            term = d[i] * moved
+                            for r in range(0, part, 8):
+                                value = term[r : r + 8]
+                                acc[t] = value if acc[t] is None else acc[t] + value
+        for t in range(25):
+            grads_ref[t : t + 1, columns] = jnp.sum(acc[t], axis=0, keepdims=True)
 
     @pl.loop(0, lanes // 128)
     def _(n):
@@ -407,24 +434,41 @@
     out_ref[at : at + left, :] = columns[:, :lanes]
     at += left
     out_ref[at:, :] = jnp.zeros((out_ref.shape[0] - at, lanes), F32)
-    heads_ref[...] = jnp.zeros_like(heads_ref)
-    heads_ref[:fields, :left] = factor_ref[:, even:]
-    out_ref[at : at + left, :128] = heads_ref[...].T[:left]
-    at += left
-    heads_ref[:fields, :1] = head_term_ref[:, lanes:]
-    out_ref[at : at + 1, :128] = heads_ref[...].T[:1]
-    at += 1
     out_ref[at : at + 1, :128] = grads_ref[:, lanes : lanes + 128].T[:1]
     at += 1
     out_ref[at : at + 1, :left] = last[:, even:]
-    at += 1
-    out_ref[at : at + 3, :] = loss_ref[:3]
     hand_out(stages()[0], pieces_ref, own_ref, [sent_ref])
 
 
-def finish_kernel(
-    count, own_one_ref, got_one_ref, own_two_ref, got_two_ref, head_ref,
-    loss_ref, kernel_ref, gain_ref, up_ref, down_ref, head_out_ref, one_ref, two_ref,
+def finish_down_kernel(count, own_ref, got_ref, head_ref, loss_ref, down_ref, head_out_ref):
+    lanes = own_ref.shape[1]
+    fields = head_ref.shape[1]
+    hidden_units = down_ref.shape[1]
+    halves = hidden_units // lanes
+    even = halves * lanes
+    left = hidden_units - even
+    span = slice(own_ref.shape[0] - EXTRA[0], own_ref.shape[0])
+    mine = place_on(stages()[0]) == 1
+    extra = jnp.where(mine, own_ref[span, :].astype(F32), got_ref[span, :].astype(F32))
+    factor = extra.astype(BF)
+    for h in range(halves):
+        down_ref[:, h * lanes : (h + 1) * lanes] = dot(
+            head_ref[...], factor[h * fields : (h + 1) * fields], ((1,), (0,))
+        )
+    at = halves * fields
+    head_out_ref[:, :lanes] = extra[at : at + fields]
+    at += fields
+    down_ref[:, even:] = dot(head_ref[...], factor[at : at + left, :fields], ((1,), (1,)))
+    tail = extra[at : at + 8].T
+    head_out_ref[:, lanes:] = tail[:fields, left : left + 1]
+    at += left + 1
+    total = extra[at : at + 1] + extra[at + 1 : at + 2] + extra[at + 2 : at + 3]
+    loss_ref[...] = jnp.sum(total, axis=1, keepdims=True) * (1.0 / count)
+
+
+def finish_up_kernel(
+    own_one_ref, got_one_ref, own_two_ref, got_two_ref,
+    kernel_ref, gain_ref, up_ref, one_ref, two_ref,
 ):
     core = place_on(stages()[0])
     for out, own, got in (
@@ -433,52 +477,38 @@
         out[core] = own[...].astype(F32)
         out[1 - core] = got[...].astype(F32)
     channels, hidden_units = up_ref.shape
-    lanes = one_ref.shape[2]
-    fields = head_ref.shape[1]
+    size, piece, lanes = one_ref.shape
     taps = kernel_ref.shape[0]
     halves = hidden_units // lanes
     even = halves * lanes
     left = hidden_units - even
     rows = 0
-    for ref in (one_ref.at[0], one_ref.at[1], two_ref.at[0], two_ref.at[1]):
-        at = 0
-        while at < ref.shape[0] and rows < even:
-            h, r = rows // lanes, rows % lanes
-            take = min(lanes - r, ref.shape[0] - at, even - rows)
-            up_ref[r : r + take, h * lanes : (h + 1) * lanes] = ref[at : at + take, :]
-            rows += take
-            at += take
-    extra = two_ref.at[1][two_ref.shape[1] - 256 :, :]
-    for h in range(halves):
-        down_ref[:, h * lanes : (h + 1) * lanes] = dot(
-            head_ref[...], extra[h * fields : (h + 1) * fields, :].astype(BF), ((1,), (0,))
-        )
-    at = halves * fields
-    head_out_ref[:, :lanes] = extra[at : at + fields]
-    at += fields
-    kernel_ref[:, :lanes] = extra[at : at + taps]
-    at += taps
-    gain_ref[:, :lanes] = extra[at : at + 1]
+    for chunk, ref in enumerate((one_ref, two_ref)):
+        for p in range(size):
+            at = 0
+            end = piece - (EXTRA[chunk] if p == size - 1 else 0)
+            while at < end:
+                h, r = rows // lanes, rows % lanes
+                take = min(lanes - r, end - at)
+                up_ref[r : r + take, h * lanes : (h + 1) * lanes] = ref[p, at : at + take, :]
+                rows += take
+                at += take
+    extra = two_ref[size - 1, piece - EXTRA[1] :, :]
+    tail = extra.T
+    kernel_ref[:, :lanes] = extra[:taps]
+    at = taps
+    gain_main = extra[at]
     at += 1
     for h in range(halves):
         up_ref[lanes:channels, h * lanes : (h + 1) * lanes] = extra[at + h : at + h + 1]
     at += halves
-    tail = extra[240:256].T
-    up_ref[:lanes, even:] = tail[:lanes, at - 240 : at - 240 + left]
+    up_ref[:lanes, even:] = tail[:lanes, at : at + left]
     at += left
-    down_ref[:, even:] = dot(
-        head_ref[...], extra[at : at + left, :fields].astype(BF), ((1,), (1,))
-    )
-    at += left
-    head_out_ref[:, lanes:] = tail[:fields, at - 240 : at - 239]
-    at += 1
-    kernel_ref[:, lanes:] = tail[:taps, at - 240 : at - 239]
-    gain_ref[:, lanes:] = extra[at : at + 1, taps : taps + 1]
+    kernel_ref[:, lanes:] = tail[:taps, at : at + 1]
+    gain_ref[:lanes] = gain_main
+    gain_ref[lanes:] = extra[at, taps : taps + 1]
     at += 1
     up_ref[lanes:channels, even:] = extra[at : at + 1, :left]
-    at += 1
-    total = extra[at : at + 1] + extra[at + 1 : at + 2] + extra[at + 2 : at + 3]
-    loss_ref[...] = jnp.sum(total, axis=1, keepdims=True) * (1.0 / count)
 
 
 def local(
@@ -530,7 +560,7 @@
         [pltpu.VMEM((height, width + 16, channels), F32), pltpu.VMEM((128, 128), F32)],
     )
     mlp = 2 * cells * channels * hidden_units
-    forecast, miss, window, normed, inverse, scaled, turned, hidden, slope, rounded = call(
+    forecast, miss, window, normed, inverse, scaled, hidden, preact, rounded = call(
         forward_kernel,
         [
             shape((nfields, cells)),
@@ -539,7 +569,6 @@
             shape((cells, channels)),
             shape((cells, 1)),
             shape((cells, channels), BF),
-            shape((channels, cells), BF),
             shape((cells, hidden_units), BF),
             shape((cells, hidden_units)),
             shape((cells, channels), BF),
@@ -552,20 +581,22 @@
         [pltpu.VMEM((cells, channels), F32)],
     )
     near = [forecast] + [swap(forecast, "mem", 2 * k) for k in order(members // 2)]
+    slope, turned = call(
+        slope_kernel,
+        [shape((cells, hidden_units)), shape((channels, cells), BF)],
+        (preact, scaled),
+        mlp,
+    )
     others = near[1:] + [swap(piece, "mem", 1) for piece in near]
     main_rows = halves * lanes
-    half = (main_rows + 256) // 4
-    small_half = half
-    own, sent, d_output, d_preact, head_term, factor, loss_rows = call(
+    half = (main_rows + sum(EXTRA)) // 4
+    own, sent, d_output, d_preact = call(
         functools.partial(score_kernel, members, bands, count),
         [
             shape((half, lanes)),
             shape((half, lanes)),
             shape((cells, channels)),
             shape((cells, hidden_units), BF),
-            shape((nfields, channels)),
-            shape((nfields, hidden_units)),
-            shape((8, lanes)),
         ],
         (
             *others, forecast, miss, weights, head_turned, down_turned, rounded, hidden, slope,
@@ -575,45 +606,51 @@
         [
             pltpu.VMEM((128, -(-cells // 128) * 128), F32),
             pltpu.VMEM((2, half, lanes), F32),
+            pltpu.VMEM((nfields, hidden_units), F32),
+            pltpu.VMEM((128, 128), F32),
         ],
     )
-    one = scatter_start(own, sent)
+    got = send(stages()[0], [sent])
+    wide, gain_row = call(
+        input_kernel,
+        [shape((cells, channels)), shape((1, channels))],
+        (d_preact, up_weight, gain, normed, inverse, d_output),
+        mlp,
+    )
+    one = sum_up([(own, *got)], stages()[1])
     first = across_plane(*one)
     own, sent = call(
         rest_kernel,
-        [shape((small_half, lanes)), shape((small_half, lanes))],
+        [shape((half, lanes)), shape((half, lanes))],
         (
-            d_preact, turned, scaled, up_weight, gain, normed, inverse, d_output, window,
-            head_term, factor, loss_rows, one[0],
+            d_preact, turned, scaled, window, wide, gain_row,
+            one[0],
         ),
         2 * mlp,
         [
-            pltpu.VMEM((cells, channels), F32),
             pltpu.VMEM((128, lanes + 128), F32),
-            pltpu.VMEM((128, 128), F32),
-            pltpu.VMEM((2, small_half, lanes), F32),
+            pltpu.VMEM((2, half, lanes), F32),
         ],
     )
     two = scatter_start(own, sent)
     second = across_plane(*two)
     one = finish_exchange(first)
     two = finish_exchange(second)
-    loss, grad_kernel, grad_gain, grad_up, grad_down, grad_head = call(
-        functools.partial(finish_kernel, count),
-        [
-            shape((1, 1)),
-            shape(conv_kernel.shape),
-            shape((1, channels)),
-            shape(up_weight.shape),
-            shape((channels, hidden_units)),
-            shape((nfields, channels)),
-        ],
-        (*one, *two, field_head_weight),
+    loss, grad_down, grad_head = call(
+        functools.partial(finish_down_kernel, count),
+        [shape((1, 1)), shape((channels, hidden_units)), shape((nfields, channels))],
+        (*one, field_head_weight),
         mlp // 4,
-        [pltpu.VMEM((2, half, lanes), F32), pltpu.VMEM((2, small_half, lanes), F32)],
+    )
+    grad_kernel, grad_gain, grad_up = call(
+        finish_up_kernel,
+        [shape(conv_kernel.shape), shape((channels,)), shape(up_weight.shape)],
+        (*one, *two),
+        mlp // 4,
+        [pltpu.VMEM((2, half, lanes), F32)] * 2,
     )
     return (
-        loss.reshape(()), grad_kernel, grad_gain[0], grad_up, grad_down.T, grad_head.T,
+        loss.reshape(()), grad_kernel, grad_gain, grad_up, grad_down.T, grad_head.T,
     )
 
 

time: 112 us -> 109 us (0.973)
  waiting for transfers between devices: 44.2 us -> 40.5 us
  local copies, waits for them, and re-layouts: 7.03 us -> 5.54 us
  Pallas kernels: 19.7 us -> 21 us
    ppermute x35, waiting for transfers between devices: 33.2 us -> 28 us  [swap(): return lax.ppermute(value, axis, [(i, i ^ mask) for i in range(count)])]
    unnamed x21 -> x19, local copies, waits for them, and re-layouts: 7.03 us -> 5.54 us
    ppermute x2, waiting for transfers between devices: 11 us -> 12.5 us  [trade(): return lax.ppermute(value, 'lat', pairs + [(j, i) for i, j in pairs])]
    pallas_call x16 -> x19, Pallas kernels: 19.7 us -> 21 us  [call(): pl.pallas_call(kernel, out_shape=outs, in_specs=[spec] * len(args), out_s...]
  transfers between devices with their start and end apart: 37 -> 37, of which waited for: 21 -> 19; matrix products, arithmetic and copies ran while one was open for 0% -> 0% of each run, Pallas kernels for 2% -> 6%
where the time goes in v1:
time: 109 us; the launch traced here: 108 us
  starting transfers between devices  40.5 us (37%)
  waiting for transfers between devices  40.5 us (37%)
  Pallas kernels  21 us (19%)
  local copies, waits for them, and re-layouts  5.54 us (5%)
    ppermute x35, starting transfers between devices, swap(): return lax.ppermute(value, axis, [(i, i ^ mask) for i in range(count)])  36.7 us
    ppermute x35, waiting for transfers between devices, swap(): return lax.ppermute(value, axis, [(i, i ^ mask) for i in range(count)])  28 us
    pallas_call x19, Pallas kernels, call(): pl.pallas_call(kernel, out_shape=outs, in_specs=[spec] * len(args), out_s...  21 us
    ppermute x2, waiting for transfers between devices, trade(): return lax.ppermute(value, 'lat', pairs + [(j, i) for i, j in pairs])  12.5 us
    unnamed x19, local copies, waits for them, and re-layouts  5.54 us
    ppermute x2, starting transfers between devices, trade(): return lax.ppermute(value, 'lat', pairs + [(j, i) for i, j in pairs])  3.79 us
  transfers between devices with their start and end apart: 37, of which 19 were waited for; matrix products, arithmetic and copies ran while one was open for 0% of the time, Pallas kernels for 6%

profile of v1, /device:TPU:0, one launch (start us, length us, event | category | flops | bytes accessed | tf_op | source)
XLA Modules:
  0.0 108.4 jit_solution(3905013405432654720)
XLA Ops:
  0.7 1.3 %copy-done.1 = f32[1,641,2,160]{1,3,2,0:T(8,128)S(1)} copy-done((f32[1,641,2,160]{1,3,2,0:T(8,128)S(1)}, f32[1,641,2,160]{1,3,2,0:T(8,128)}, u32[]{:S(2)}) %copy-start.1) | copy-done | bytes 820504
  2.0 0.2 shard_map.128
  2.1 3.1 %collective-permute-start = (f32[328,640]{1,0:T(8,128)S(1)}, f32[328,640]{1,0:T(8,128)S(1)}, u32[]{:S(2)}, u32[]{:S(2)}) collective-permute-start(f32[328,640]{1,0:T(8,128)S(1)} %shard_map.128), channel_id=1, source_target_pairs={{0,1},{2,3},{1,0},{3,2},{4,5},{6,7},{5,4},{7,6},{8,9},{10,11},{9,8... | collective-permute-start | bytes 2519048 | tf_op jit(solution)/shard_map/ppermute | solution.py:539
  5.2 0.7 collective-permute-start.1
  6.0 0.9 copy-done.3
  6.8 0.9 copy-done.5
  7.7 0.9 copy-done.6
  8.6 0.7 copy-done.7
  9.3 0.7 copy-done.8
  10.0 1.4 %shard_map.127 = (f32[320,641]{1,0:T(8,128)S(1)}, f32[1,641]{1,0:T(1,128)S(1)}, f32[72,320]{1,0:T(8,128)S(1)}, f32[72,320]{1,0:T(8,128)S(1)}) custom-call(f32[2,160,641]{2,1,0:T(8,128)S(1)} %bitcast.13, f32[25,641]{1,0:T(8,128)S(1)} %copy-done.5, f32[641]{0:T(1024)S(1)} %copy-done.7, f32[72,2,160]{2,1,0:T(2,128)S(1)} %copy-done.6, f32[72]{0:T(128)S(1)} %copy-done.8, ...), custom_call_target="tpu_custom_call" | custom-call | flops 100000000 | bytes 3722784 | tf_op jit(solution)/shard_map/pallas_call | solution.py:125
  11.4 12.5 %collective-permute-done.first_ref = f32[328,640]{1,0:T(8,128)S(1)} collective-permute-done((f32[328,640]{1,0:T(8,128)S(1)}, f32[328,640]{1,0:T(8,128)S(1)}, u32[]{:S(2)}, u32[]{:S(2)}) %collective-permute-start) | collective-permute-done | bytes 839712 | tf_op jit(solution)/shard_map/ppermute | solution.py:539
  23.9 5.0 %shard_map.129 = (f32[72,320]{1,0:T(8,128)S(1)}, f32[72,320]{1,0:T(8,128)S(1)}, f32[6,176,641]{2,1,0:T(8,128)S(1)}, f32[320,641]{1,0:T(8,128)S(1)}, f32[320,1]{1...) custom-call(f32[2,160,641]{2,1,0:T(8,128)S(1)} %bitcast.14, ...), custom_call_target="tpu_custom_call" | custom-call | flops 1051855360 | bytes 13854080 | tf_op jit(solution)/shard_map/pallas_call | solution.py:125
  28.9 2.7 %collective-permute-start.2 = (f32[72,320]{1,0:T(8,128)S(1)}, f32[72,320]{1,0:T(8,128)S(1)}, u32[]{:S(2)}, u32[]{:S(2)}) collective-permute-start(f32[72,320]{1,0:T(8,128)S(1)} %get-tuple-element.54.refs_7_), channel_id=1, source_target_pairs={{0,24},{4,28},{8,16},{12,20},{16,8},{20,12},{24,0},{28,4},{1,25},{... | collective-permute-start | bytes 276488 | tf_op jit(solution)/shard_map/ppermute | solution.py:25
  31.6 0.5 collective-permute-start.3
  32.1 0.3 collective-permute-start.4
  32.5 2.9 %collective-permute-done.2.refs_0_ = f32[72,320]{1,0:T(8,128)S(1)} collective-permute-done((f32[72,320]{1,0:T(8,128)S(1)}, f32[72,320]{1,0:T(8,128)S(1)}, u32[]{:S(2)}, u32[]{:S(2)}) %collective-permute-start.2) | collective-permute-done | bytes 92192 | tf_op jit(solution)/shard_map/ppermute | solution.py:25
  35.4 1.0 collective-permute-done.3.refs_1_
  36.5 0.4 collective-permute-done.4.refs_2_
  37.0 1.1 %shard_map.130 = (f32[320,1282]{1,0:T(8,128)S(1)}, bf16[641,320]{1,0:T(8,128)(2,1)S(1)}) custom-call(f32[320,1282]{1,0:T(8,128)S(1)} %get-tuple-element.59.preact_ref, bf16[320,641]{1,0:T(8,128)(2,1)S(1)} %get-tuple-element.60.scaled_ref), custom_call_target="tpu_custom_call" | custom-call | flops 525927680 | bytes 4102400 | tf_op jit(solution)/shard_map/pallas_call | solution.py:125
  38.2 2.2 %shard_map.131 = (f32[384,640]{1,0:T(8,128)S(1)}, f32[384,640]{1,0:T(8,128)S(1)}, f32[320,641]{1,0:T(8,128)S(1)}, bf16[320,1282]{1,0:T(8,128)(2,1)S(1)}) custom-call(f32[72,320]{1,0:T(8,128)S(1)} %collective-permute-done.2.refs_0_, f32[72,320]{1,0:T(8,128)S(1)} %collective-permute-done.3.refs_1_, f32[72,320]{1,0:T(8,128)S(1)} %collective-permute-done.4.refs_2_, ...), custom_call_target="tpu_custom_call" | custom-call | flops 1051855360 | bytes 9546388 | tf_op jit(solution)/shard_map/pallas_call | solution.py:125
  40.4 0.4 collective-permute-start.9
  40.9 1.3 %shard_map.138 = (f32[320,641]{1,0:T(8,128)S(1)}, f32[1,641]{1,0:T(1,128)S(1)}) custom-call(bf16[320,1282]{1,0:T(8,128)(2,1)S(1)} %get-tuple-element.74.preact_ref, bf16[641,1282]{1,0:T(8,128)(2,1)S(1)} %copy-done, f32[1,641]{1,0:T(1,128)S(1)} %get-tuple-element.52.gain_ref, f32[320,641]{1,0:T(8,128)S(1)} %get-tuple-element.76.normed_ref, ...), custom_call_target="tpu_custom_call" | custom-call | flops 525927680 | bytes 4931852 | tf_op jit(solution)/shard_map/pallas_call | solution.py:125
  42.2 0.9 collective-permute-done.9.refs_1_
  43.1 0.2 shard_map.132
  43.2 4.0 %shard_map.139 = (f32[384,640]{1,0:T(8,128)S(1)}, f32[384,640]{1,0:T(8,128)S(1)}) custom-call(bf16[320,1282]{1,0:T(8,128)(2,1)S(1)} %get-tuple-element.74.preact_ref, bf16[641,320]{1,0:T(8,128)(2,1)S(1)} %get-tuple-element.62.refs_15_.turned_ref, bf16[320,641]{1,0:T(8,128)(2,1)S(1)} %get-tuple-element.60.scaled_ref, ...), custom_call_target="tpu_custom_call" | custom-call | flops 1051855360 | bytes 7383428 | tf_op jit(solution)/shard_map/pallas_call | solution.py:125
  47.2 0.4 collective-permute-start.23
  47.6 1.9 %collective-permute-start.10 = (bf16[96,640]{1,0:T(8,128)(2,1)S(1)}, bf16[96,640]{1,0:T(8,128)(2,1)S(1)}, u32[]{:S(2)}, u32[]{:S(2)}) collective-permute-start(bf16[96,640]{1,0:T(8,128)(2,1)S(1)} %get-tuple-element.66), channel_id=1, source_target_pairs={{0,24},{4,28},{8,16},{12,20},{16,8},{20,12},{24,0},{28,4},{1,25},{... | collective-permute-start | bytes 368648 | tf_op jit(solution)/shard_map/ppermute | solution.py:25
  49.6 0.6 collective-permute-start.11
  50.1 1.0 collective-permute-start.12
  51.1 3.6 %collective-permute-done.10.refs_1_ = bf16[96,640]{1,0:T(8,128)(2,1)S(1)} collective-permute-done((bf16[96,640]{1,0:T(8,128)(2,1)S(1)}, bf16[96,640]{1,0:T(8,128)(2,1)S(1)}, u32[]{:S(2)}, u32[]{:S(2)}) %collective-permute-start.10) | collective-permute-done | bytes 122912 | tf_op jit(solution)/shard_map/ppermute | solution.py:25
  54.7 1.4 %collective-permute-done.11.refs_2_ = bf16[96,640]{1,0:T(8,128)(2,1)S(1)} collective-permute-done((bf16[96,640]{1,0:T(8,128)(2,1)S(1)}, bf16[96,640]{1,0:T(8,128)(2,1)S(1)}, u32[]{:S(2)}, u32[]{:S(2)}) %collective-permute-start.11) | collective-permute-done | bytes 122912 | tf_op jit(solution)/shard_map/ppermute | solution.py:25
  56.1 0.4 collective-permute-done.12.refs_3_
  56.6 3.7 %collective-permute-start.13 = (bf16[24,640]{1,0:T(8,128)(2,1)S(1)}, bf16[24,640]{1,0:T(8,128)(2,1)S(1)}, u32[]{:S(2)}, u32[]{:S(2)}) collective-permute-start(bf16[24,640]{1,0:T(8,128)(2,1)S(1)} %get-tuple-element.70), channel_id=1, source_target_pairs={{0,3},{1,2},{2,1},{3,0},{4,7},{5,6},{6,5},{7,4},{8,11},{9,10},{10,... | collective-permute-start | bytes 92168 | tf_op jit(solution)/shard_map/ppermute | solution.py:25
  60.3 2.7 %collective-permute-start.14 = (bf16[24,640]{1,0:T(8,128)(2,1)S(1)}, bf16[24,640]{1,0:T(8,128)(2,1)S(1)}, u32[]{:S(2)}, u32[]{:S(2)}) collective-permute-start(bf16[24,640]{1,0:T(8,128)(2,1)S(1)} %get-tuple-element.71), channel_id=1, source_target_pairs={{0,1},{1,0},{2,3},{3,2},{4,5},{5,4},{6,7},{7,6},{8,9},{9,8},{10,11... | collective-permute-start | bytes 92168 | tf_op jit(solution)/shard_map/ppermute | solution.py:25
  63.0 0.2 shard_map.140
  63.2 1.7 %collective-permute-start.24 = (bf16[96,640]{1,0:T(8,128)(2,1)S(1)}, bf16[96,640]{1,0:T(8,128)(2,1)S(1)}, u32[]{:S(2)}, u32[]{:S(2)}) collective-permute-start(bf16[96,640]{1,0:T(8,128)(2,1)S(1)} %get-tuple-element.84), channel_id=1, source_target_pairs={{0,24},{4,28},{8,16},{12,20},{16,8},{20,12},{24,0},{28,4},{1,25},{... | collective-permute-start | bytes 368648 | tf_op jit(solution)/shard_map/ppermute | solution.py:25
  64.9 0.6 collective-permute-start.25
  65.5 1.3 %collective-permute-start.26 = (bf16[96,640]{1,0:T(8,128)(2,1)S(1)}, bf16[96,640]{1,0:T(8,128)(2,1)S(1)}, u32[]{:S(2)}, u32[]{:S(2)}) collective-permute-start(bf16[96,640]{1,0:T(8,128)(2,1)S(1)} %get-tuple-element.86), channel_id=1, source_target_pairs={{0,16},{4,20},{8,24},{12,28},{16,0},{20,4},{24,8},{28,12},{1,17},{... | collective-permute-start | bytes 368648 | tf_op jit(solution)/shard_map/ppermute | solution.py:25
  66.8 1.1 collective-permute-done.15.refs_3_
  67.8 1.6 %collective-permute-start.16 = (bf16[24,640]{1,0:T(8,128)(2,1)S(1)}, bf16[24,640]{1,0:T(8,128)(2,1)S(1)}, u32[]{:S(2)}, u32[]{:S(2)}) collective-permute-start(bf16[24,640]{1,0:T(8,128)(2,1)S(1)} %shard_map.134.own_ref), channel_id=1, source_target_pairs={{0,3},{1,2},{2,1},{3,0},{4,7},{5,6},{6,5},{7,4},{8,11},{9,10},{10,... | collective-permute-start | bytes 92168 | tf_op jit(solution)/shard_map/ppermute | solution.py:25
  69.4 0.9 collective-permute-start.17
  70.3 3.5 %collective-permute-done.16.refs_0_ = bf16[24,640]{1,0:T(8,128)(2,1)S(1)} collective-permute-done((bf16[24,640]{1,0:T(8,128)(2,1)S(1)}, bf16[24,640]{1,0:T(8,128)(2,1)S(1)}, u32[]{:S(2)}, u32[]{:S(2)}) %collective-permute-start.16) | collective-permute-done | bytes 30752 | tf_op jit(solution)/shard_map/ppermute | solution.py:25
  73.9 4.8 %collective-permute-done.18.refs_2_ = bf16[24,640]{1,0:T(8,128)(2,1)S(1)} collective-permute-done((bf16[24,640]{1,0:T(8,128)(2,1)S(1)}, bf16[24,640]{1,0:T(8,128)(2,1)S(1)}, u32[]{:S(2)}, u32[]{:S(2)}) %collective-permute-start.18) | collective-permute-done | bytes 30752 | tf_op jit(solution)/shard_map/ppermute | solution.py:25
  78.7 1.7 %collective-permute-start.19 = (bf16[96,640]{1,0:T(8,128)(2,1)S(1)}, bf16[96,640]{1,0:T(8,128)(2,1)S(1)}, u32[]{:S(2)}, u32[]{:S(2)}) collective-permute-start(bf16[96,640]{1,0:T(8,128)(2,1)S(1)} %bitcast.25), channel_id=1, source_target_pairs={{0,24},{4,28},{8,16},{12,20},{16,8},{20,12},{24,0},{28,4},{1,25},{... | collective-permute-start | bytes 368648 | tf_op jit(solution)/shard_map/ppermute | solution.py:25
  80.5 1.6 %collective-permute-start.27 = (bf16[24,640]{1,0:T(8,128)(2,1)S(1)}, bf16[24,640]{1,0:T(8,128)(2,1)S(1)}, u32[]{:S(2)}, u32[]{:S(2)}) collective-permute-start(bf16[24,640]{1,0:T(8,128)(2,1)S(1)} %get-tuple-element.88), channel_id=1, source_target_pairs={{0,3},{1,2},{2,1},{3,0},{4,7},{5,6},{6,5},{7,4},{8,11},{9,10},{10,... | collective-permute-start | bytes 92168 | tf_op jit(solution)/shard_map/ppermute | solution.py:25
  82.1 2.8 %collective-permute-start.29 = (bf16[24,640]{1,0:T(8,128)(2,1)S(1)}, bf16[24,640]{1,0:T(8,128)(2,1)S(1)}, u32[]{:S(2)}, u32[]{:S(2)}) collective-permute-start(bf16[24,640]{1,0:T(8,128)(2,1)S(1)} %get-tuple-element.90), channel_id=1, source_target_pairs={{0,2},{1,3},{2,0},{3,1},{4,6},{5,7},{6,4},{7,5},{8,10},{9,11},{10,... | collective-permute-start | bytes 92168 | tf_op jit(solution)/shard_map/ppermute | solution.py:25
  85.0 1.4 %collective-permute-done.27.refs_1_ = bf16[24,640]{1,0:T(8,128)(2,1)S(1)} collective-permute-done((bf16[24,640]{1,0:T(8,128)(2,1)S(1)}, bf16[24,640]{1,0:T(8,128)(2,1)S(1)}, u32[]{:S(2)}, u32[]{:S(2)}) %collective-permute-start.27) | collective-permute-done | bytes 30752 | tf_op jit(solution)/shard_map/ppermute | solution.py:25
  86.3 0.7 collective-permute-done.28.refs_2_
  87.1 2.3 %collective-permute-start.30 = (bf16[24,640]{1,0:T(8,128)(2,1)S(1)}, bf16[24,640]{1,0:T(8,128)(2,1)S(1)}, u32[]{:S(2)}, u32[]{:S(2)}) collective-permute-start(bf16[24,640]{1,0:T(8,128)(2,1)S(1)} %shard_map.142.own_ref), channel_id=1, source_target_pairs={{0,3},{1,2},{2,1},{3,0},{4,7},{5,6},{6,5},{7,4},{8,11},{9,10},{10,... | collective-permute-start | bytes 92168 | tf_op jit(solution)/shard_map/ppermute | solution.py:25
  89.4 1.0 collective-permute-start.31
  90.4 1.1 %collective-permute-start.32 = (bf16[24,640]{1,0:T(8,128)(2,1)S(1)}, bf16[24,640]{1,0:T(8,128)(2,1)S(1)}, u32[]{:S(2)}, u32[]{:S(2)}) collective-permute-start(bf16[24,640]{1,0:T(8,128)(2,1)S(1)} %shard_map.142.own_ref), channel_id=1, source_target_pairs={{0,2},{1,3},{2,0},{3,1},{4,6},{5,7},{6,4},{7,5},{8,10},{9,11},{10,... | collective-permute-start | bytes 92168 | tf_op jit(solution)/shard_map/ppermute | solution.py:25
  91.5 0.8 collective-permute-start.20
  92.3 0.5 collective-permute-done.30.refs_0_
  92.8 1.2 %collective-permute-start.21 = (bf16[96,640]{1,0:T(8,128)(2,1)S(1)}, bf16[96,640]{1,0:T(8,128)(2,1)S(1)}, u32[]{:S(2)}, u32[]{:S(2)}) collective-permute-start(bf16[96,640]{1,0:T(8,128)(2,1)S(1)} %bitcast.27), channel_id=1, source_target_pairs={{0,16},{4,20},{8,24},{12,28},{16,0},{20,4},{24,8},{28,12},{1,17},{... | collective-permute-start | bytes 368648 | tf_op jit(solution)/shard_map/ppermute | solution.py:25
  94.0 1.2 %collective-permute-done.32.refs_2_ = bf16[24,640]{1,0:T(8,128)(2,1)S(1)} collective-permute-done((bf16[24,640]{1,0:T(8,128)(2,1)S(1)}, bf16[24,640]{1,0:T(8,128)(2,1)S(1)}, u32[]{:S(2)}, u32[]{:S(2)}) %collective-permute-start.32) | collective-permute-done | bytes 30752 | tf_op jit(solution)/shard_map/ppermute | solution.py:25
  95.2 1.3 %collective-permute-start.33 = (bf16[96,640]{1,0:T(8,128)(2,1)S(1)}, bf16[96,640]{1,0:T(8,128)(2,1)S(1)}, u32[]{:S(2)}, u32[]{:S(2)}) collective-permute-start(bf16[96,640]{1,0:T(8,128)(2,1)S(1)} %bitcast.29), channel_id=1, source_target_pairs={{0,24},{4,28},{8,16},{12,20},{16,8},{20,12},{24,0},{28,4},{1,25},{... | collective-permute-start | bytes 368648 | tf_op jit(solution)/shard_map/ppermute | solution.py:25
  96.6 1.5 %collective-permute-start.34 = (bf16[96,640]{1,0:T(8,128)(2,1)S(1)}, bf16[96,640]{1,0:T(8,128)(2,1)S(1)}, u32[]{:S(2)}, u32[]{:S(2)}) collective-permute-start(bf16[96,640]{1,0:T(8,128)(2,1)S(1)} %bitcast.30), channel_id=1, source_target_pairs={{0,8},{4,12},{8,0},{12,4},{16,24},{20,28},{24,16},{28,20},{1,9},{5... | collective-permute-start | bytes 368648 | tf_op jit(solution)/shard_map/ppermute | solution.py:25
  98.0 0.7 collective-permute-start.35
  98.9 2.1 %collective-permute-done.33.refs_0_ = bf16[96,640]{1,0:T(8,128)(2,1)S(1)} collective-permute-done((bf16[96,640]{1,0:T(8,128)(2,1)S(1)}, bf16[96,640]{1,0:T(8,128)(2,1)S(1)}, u32[]{:S(2)}, u32[]{:S(2)}) %collective-permute-start.33) | collective-permute-done | bytes 122912 | tf_op jit(solution)/shard_map/ppermute | solution.py:25
  101.1 1.2 %collective-permute-done.34.refs_1_ = bf16[96,640]{1,0:T(8,128)(2,1)S(1)} collective-permute-done((bf16[96,640]{1,0:T(8,128)(2,1)S(1)}, bf16[96,640]{1,0:T(8,128)(2,1)S(1)}, u32[]{:S(2)}, u32[]{:S(2)}) %collective-permute-start.34) | collective-permute-done | bytes 122912 | tf_op jit(solution)/shard_map/ppermute | solution.py:25
  102.2 0.7 collective-permute-done.35.refs_2_
  103.1 0.2 copy.14.head_ref
  103.3 2.7 %shard_map.137 = (f32[1,1]{1,0:T(1,128)}, f32[641,1282]{1,0:T(8,128)}, f32[72,641]{1,0:T(8,128)}) custom-call(bf16[384,640]{1,0:T(8,128)(2,1)S(1)} %bitcast.18, bf16[384,640]{1,0:T(8,128)(2,1)S(1)} %collective-permute-done.22.got_ref.got_one_ref, bf16[641,72]{1,0:T(8,128)(2,1)S(1)} %copy.14.head_ref), custom_call_target="tpu_custom_call" | custom-call | flops 131481920 | bytes 4547004 | tf_op jit(solution)/shard_map/pallas_call | solution.py:125
  105.9 2.5 %shard_map.145 = (f32[25,641]{1,0:T(8,128)}, f32[641]{0:T(1024)}, f32[641,1282]{1,0:T(8,128)}) custom-call(bf16[384,640]{1,0:T(8,128)(2,1)S(1)} %bitcast.19, bf16[384,640]{1,0:T(8,128)(2,1)S(1)} %collective-permute-done.22.got_ref.got_one_ref, bf16[384,640]{1,0:T(8,128)(2,1)S(1)} %bitcast.21, bf16[384,640]{1,0:T(8,128)(2,1)S(1)} %collective-permute-done.36.got_two_ref), custom_call_target="tpu_custom_call" | custom-call | flops 131481920 | bytes 5319792 | tf_op jit(solution)/shard_map/pallas_call | solution.py:125
  (48 shorter events, 0.8 us)
Async XLA Ops:
  0.6 5.3 %copy-start = (bf16[641,1282]{1,0:T(8,128)(2,1)S(1)}, bf16[641,1282]{1,0:T(8,128)(2,1)}, u32[]{:S(2)}) copy-start(bf16[641,1282]{1,0:T(8,128)(2,1)} %up_ref.3) | copy-start | bytes 4930576
  0.6 1.3 %copy-start.1 = (f32[1,641,2,160]{1,3,2,0:T(8,128)S(1)}, f32[1,641,2,160]{1,3,2,0:T(8,128)}, u32[]{:S(2)}) copy-start(f32[1,641,2,160]{1,3,2,0:T(8,128)} %param.8) | copy-start | bytes 2461444
  2.1 21.8 %copy-start.2 = (bf16[1282,641]{0,1:T(8,128)(2,1)S(1)}, bf16[1282,641]{0,1:T(8,128)(2,1)}, u32[]{:S(2)}) copy-start(bf16[1282,641]{0,1:T(8,128)(2,1)} %param.12) | copy-start | bytes 4930576
  2.1 21.8 %collective-permute-start = (f32[328,640]{1,0:T(8,128)S(1)}, f32[328,640]{1,0:T(8,128)S(1)}, u32[]{:S(2)}, u32[]{:S(2)}) collective-permute-start(f32[328,640]{1,0:T(8,128)S(1)} %shard_map.128), channel_id=1, source_target_pairs={{0,1},{2,3},{1,0},{3,2},{4,5},{6,7},{5,4},{7,6},{8,9},{10,11},{9,8... | collective-permute-start | bytes 2519048 | tf_op jit(solution)/shard_map/ppermute | solution.py:539
  5.2 18.7 %collective-permute-start.1 = (f32[328,640]{1,0:T(8,128)S(1)}, f32[328,640]{1,0:T(8,128)S(1)}, u32[]{:S(2)}, u32[]{:S(2)}) collective-permute-start(f32[328,640]{1,0:T(8,128)S(1)} %shard_map.128), channel_id=1, source_target_pairs={{1,2},{2,1},{5,6},{6,5},{9,10},{10,9},{13,14},{14,13},{17,18},{18,... | collective-permute-start | bytes 2519048 | tf_op jit(solution)/shard_map/ppermute | solution.py:539
  5.9 0.9 copy-start.3
  6.8 0.9 copy-start.5
  7.7 0.9 copy-start.6
  8.6 0.7 copy-start.7
  9.3 0.7 copy-start.8
  28.9 6.5 %collective-permute-start.2 = (f32[72,320]{1,0:T(8,128)S(1)}, f32[72,320]{1,0:T(8,128)S(1)}, u32[]{:S(2)}, u32[]{:S(2)}) collective-permute-start(f32[72,320]{1,0:T(8,128)S(1)} %get-tuple-element.54.refs_7_), channel_id=1, source_target_pairs={{0,24},{4,28},{8,16},{12,20},{16,8},{20,12},{24,0},{28,4},{1,25},{... | collective-permute-start | bytes 276488 | tf_op jit(solution)/shard_map/ppermute | solution.py:25
  31.6 4.8 %collective-permute-start.3 = (f32[72,320]{1,0:T(8,128)S(1)}, f32[72,320]{1,0:T(8,128)S(1)}, u32[]{:S(2)}, u32[]{:S(2)}) collective-permute-start(f32[72,320]{1,0:T(8,128)S(1)} %get-tuple-element.54.refs_7_), channel_id=1, source_target_pairs={{0,8},{4,12},{8,0},{12,4},{16,24},{20,28},{24,16},{28,20},{1,9},{5... | collective-permute-start | bytes 276488 | tf_op jit(solution)/shard_map/ppermute | solution.py:25
  32.1 4.7 %collective-permute-start.4 = (f32[72,320]{1,0:T(8,128)S(1)}, f32[72,320]{1,0:T(8,128)S(1)}, u32[]{:S(2)}, u32[]{:S(2)}) collective-permute-start(f32[72,320]{1,0:T(8,128)S(1)} %get-tuple-element.54.refs_7_), channel_id=1, source_target_pairs={{0,16},{4,20},{8,24},{12,28},{16,0},{20,4},{24,8},{28,12},{1,17},{... | collective-permute-start | bytes 276488 | tf_op jit(solution)/shard_map/ppermute | solution.py:25
  32.5 5.6 %collective-permute-start.5 = (f32[72,320]{1,0:T(8,128)S(1)}, f32[72,320]{1,0:T(8,128)S(1)}, u32[]{:S(2)}, u32[]{:S(2)}) collective-permute-start(f32[72,320]{1,0:T(8,128)S(1)} %get-tuple-element.54.refs_7_), channel_id=1, source_target_pairs={{0,4},{4,0},{8,12},{12,8},{16,20},{20,16},{24,28},{28,24},{1,5},{5... | collective-permute-start | bytes 276488 | tf_op jit(solution)/shard_map/ppermute | solution.py:25
  35.4 2.7 %collective-permute-start.6 = (f32[72,320]{1,0:T(8,128)S(1)}, f32[72,320]{1,0:T(8,128)S(1)}, u32[]{:S(2)}, u32[]{:S(2)}) collective-permute-start(f32[72,320]{1,0:T(8,128)S(1)} %collective-permute-done.2.refs_0_), channel_id=1, source_target_pairs={{0,4},{4,0},{8,12},{12,8},{16,20},{20,16},{24,28},{28,24},{1,5},{5... | collective-permute-start | bytes 276488 | tf_op jit(solution)/shard_map/ppermute | solution.py:25
  36.5 1.7 %collective-permute-start.7 = (f32[72,320]{1,0:T(8,128)S(1)}, f32[72,320]{1,0:T(8,128)S(1)}, u32[]{:S(2)}, u32[]{:S(2)}) collective-permute-start(f32[72,320]{1,0:T(8,128)S(1)} %collective-permute-done.3.refs_1_), channel_id=1, source_target_pairs={{0,4},{4,0},{8,12},{12,8},{16,20},{20,16},{24,28},{28,24},{1,5},{5... | collective-permute-start | bytes 276488 | tf_op jit(solution)/shard_map/ppermute | solution.py:25
  36.9 1.3 %collective-permute-start.8 = (f32[72,320]{1,0:T(8,128)S(1)}, f32[72,320]{1,0:T(8,128)S(1)}, u32[]{:S(2)}, u32[]{:S(2)}) collective-permute-start(f32[72,320]{1,0:T(8,128)S(1)} %collective-permute-done.4.refs_2_), channel_id=1, source_target_pairs={{0,4},{4,0},{8,12},{12,8},{16,20},{20,16},{24,28},{28,24},{1,5},{5... | collective-permute-start | bytes 276488 | tf_op jit(solution)/shard_map/ppermute | solution.py:25
  40.4 2.6 %collective-permute-start.9 = (f32[384,640]{1,0:T(8,128)S(1)}, f32[384,640]{1,0:T(8,128)S(1)}, u32[]{:S(2)}, u32[]{:S(2)}) collective-permute-start(f32[384,640]{1,0:T(8,128)S(1)} %get-tuple-element.64), channel_id=1, source_target_pairs={{0,4},{4,0},{8,12},{12,8},{16,20},{20,16},{24,28},{28,24},{1,5},{5... | collective-permute-start | bytes 2949128 | tf_op jit(solution)/shard_map/ppermute | solution.py:25
  47.2 15.8 %collective-permute-start.23 = (f32[384,640]{1,0:T(8,128)S(1)}, f32[384,640]{1,0:T(8,128)S(1)}, u32[]{:S(2)}, u32[]{:S(2)}) collective-permute-start(f32[384,640]{1,0:T(8,128)S(1)} %get-tuple-element.82), channel_id=1, source_target_pairs={{0,4},{4,0},{8,12},{12,8},{16,20},{20,16},{24,28},{28,24},{1,5},{5... | collective-permute-start | bytes 2949128 | tf_op jit(solution)/shard_map/ppermute | solution.py:25
  47.6 7.1 %collective-permute-start.10 = (bf16[96,640]{1,0:T(8,128)(2,1)S(1)}, bf16[96,640]{1,0:T(8,128)(2,1)S(1)}, u32[]{:S(2)}, u32[]{:S(2)}) collective-permute-start(bf16[96,640]{1,0:T(8,128)(2,1)S(1)} %get-tuple-element.66), channel_id=1, source_target_pairs={{0,24},{4,28},{8,16},{12,20},{16,8},{20,12},{24,0},{28,4},{1,25},{... | collective-permute-start | bytes 368648 | tf_op jit(solution)/shard_map/ppermute | solution.py:25
  49.6 6.5 %collective-permute-start.11 = (bf16[96,640]{1,0:T(8,128)(2,1)S(1)}, bf16[96,640]{1,0:T(8,128)(2,1)S(1)}, u32[]{:S(2)}, u32[]{:S(2)}) collective-permute-start(bf16[96,640]{1,0:T(8,128)(2,1)S(1)} %get-tuple-element.67), channel_id=1, source_target_pairs={{0,8},{4,12},{8,0},{12,4},{16,24},{20,28},{24,16},{28,20},{1,9},{5... | collective-permute-start | bytes 368648 | tf_op jit(solution)/shard_map/ppermute | solution.py:25
  50.1 6.4 %collective-permute-start.12 = (bf16[96,640]{1,0:T(8,128)(2,1)S(1)}, bf16[96,640]{1,0:T(8,128)(2,1)S(1)}, u32[]{:S(2)}, u32[]{:S(2)}) collective-permute-start(bf16[96,640]{1,0:T(8,128)(2,1)S(1)} %get-tuple-element.68), channel_id=1, source_target_pairs={{0,16},{4,20},{8,24},{12,28},{16,0},{20,4},{24,8},{28,12},{1,17},{... | collective-permute-start | bytes 368648 | tf_op jit(solution)/shard_map/ppermute | solution.py:25
  56.6 8.9 %collective-permute-start.13 = (bf16[24,640]{1,0:T(8,128)(2,1)S(1)}, bf16[24,640]{1,0:T(8,128)(2,1)S(1)}, u32[]{:S(2)}, u32[]{:S(2)}) collective-permute-start(bf16[24,640]{1,0:T(8,128)(2,1)S(1)} %get-tuple-element.70), channel_id=1, source_target_pairs={{0,3},{1,2},{2,1},{3,0},{4,7},{5,6},{6,5},{7,4},{8,11},{9,10},{10,... | collective-permute-start | bytes 92168 | tf_op jit(solution)/shard_map/ppermute | solution.py:25
  60.3 6.5 %collective-permute-start.14 = (bf16[24,640]{1,0:T(8,128)(2,1)S(1)}, bf16[24,640]{1,0:T(8,128)(2,1)S(1)}, u32[]{:S(2)}, u32[]{:S(2)}) collective-permute-start(bf16[24,640]{1,0:T(8,128)(2,1)S(1)} %get-tuple-element.71), channel_id=1, source_target_pairs={{0,1},{1,0},{2,3},{3,2},{4,5},{5,4},{6,7},{7,6},{8,9},{9,8},{10,11... | collective-permute-start | bytes 92168 | tf_op jit(solution)/shard_map/ppermute | solution.py:25
  63.0 4.8 %collective-permute-start.15 = (bf16[24,640]{1,0:T(8,128)(2,1)S(1)}, bf16[24,640]{1,0:T(8,128)(2,1)S(1)}, u32[]{:S(2)}, u32[]{:S(2)}) collective-permute-start(bf16[24,640]{1,0:T(8,128)(2,1)S(1)} %get-tuple-element.72), channel_id=1, source_target_pairs={{0,2},{1,3},{2,0},{3,1},{4,6},{5,7},{6,4},{7,5},{8,10},{9,11},{10,... | collective-permute-start | bytes 92168 | tf_op jit(solution)/shard_map/ppermute | solution.py:25
  63.2 39.9 %copy-start.4 = (bf16[641,72]{0,1:T(8,128)(2,1)S(1)}, bf16[641,72]{0,1:T(8,128)(2,1)}, u32[]{:S(2)}) copy-start(bf16[641,72]{0,1:T(8,128)(2,1)} %param.13) | copy-start | bytes 276916
  63.2 17.2 %collective-permute-start.24 = (bf16[96,640]{1,0:T(8,128)(2,1)S(1)}, bf16[96,640]{1,0:T(8,128)(2,1)S(1)}, u32[]{:S(2)}, u32[]{:S(2)}) collective-permute-start(bf16[96,640]{1,0:T(8,128)(2,1)S(1)} %get-tuple-element.84), channel_id=1, source_target_pairs={{0,24},{4,28},{8,16},{12,20},{16,8},{20,12},{24,0},{28,4},{1,25},{... | collective-permute-start | bytes 368648 | tf_op jit(solution)/shard_map/ppermute | solution.py:25
  64.9 15.5 %collective-permute-start.25 = (bf16[96,640]{1,0:T(8,128)(2,1)S(1)}, bf16[96,640]{1,0:T(8,128)(2,1)S(1)}, u32[]{:S(2)}, u32[]{:S(2)}) collective-permute-start(bf16[96,640]{1,0:T(8,128)(2,1)S(1)} %get-tuple-element.85), channel_id=1, source_target_pairs={{0,8},{4,12},{8,0},{12,4},{16,24},{20,28},{24,16},{28,20},{1,9},{5... | collective-permute-start | bytes 368648 | tf_op jit(solution)/shard_map/ppermute | solution.py:25
  65.5 14.9 %collective-permute-start.26 = (bf16[96,640]{1,0:T(8,128)(2,1)S(1)}, bf16[96,640]{1,0:T(8,128)(2,1)S(1)}, u32[]{:S(2)}, u32[]{:S(2)}) collective-permute-start(bf16[96,640]{1,0:T(8,128)(2,1)S(1)} %get-tuple-element.86), channel_id=1, source_target_pairs={{0,16},{4,20},{8,24},{12,28},{16,0},{20,4},{24,8},{28,12},{1,17},{... | collective-permute-start | bytes 368648 | tf_op jit(solution)/shard_map/ppermute | solution.py:25
  67.8 6.0 %collective-permute-start.16 = (bf16[24,640]{1,0:T(8,128)(2,1)S(1)}, bf16[24,640]{1,0:T(8,128)(2,1)S(1)}, u32[]{:S(2)}, u32[]{:S(2)}) collective-permute-start(bf16[24,640]{1,0:T(8,128)(2,1)S(1)} %shard_map.134.own_ref), channel_id=1, source_target_pairs={{0,3},{1,2},{2,1},{3,0},{4,7},{5,6},{6,5},{7,4},{8,11},{9,10},{10,... | collective-permute-start | bytes 92168 | tf_op jit(solution)/shard_map/ppermute | solution.py:25
  69.4 4.5 %collective-permute-start.17 = (bf16[24,640]{1,0:T(8,128)(2,1)S(1)}, bf16[24,640]{1,0:T(8,128)(2,1)S(1)}, u32[]{:S(2)}, u32[]{:S(2)}) collective-permute-start(bf16[24,640]{1,0:T(8,128)(2,1)S(1)} %shard_map.134.own_ref), channel_id=1, source_target_pairs={{0,1},{1,0},{2,3},{3,2},{4,5},{5,4},{6,7},{7,6},{8,9},{9,8},{10,11... | collective-permute-start | bytes 92168 | tf_op jit(solution)/shard_map/ppermute | solution.py:25
  73.9 4.8 %collective-permute-start.18 = (bf16[24,640]{1,0:T(8,128)(2,1)S(1)}, bf16[24,640]{1,0:T(8,128)(2,1)S(1)}, u32[]{:S(2)}, u32[]{:S(2)}) collective-permute-start(bf16[24,640]{1,0:T(8,128)(2,1)S(1)} %shard_map.134.own_ref), channel_id=1, source_target_pairs={{0,2},{1,3},{2,0},{3,1},{4,6},{5,7},{6,4},{7,5},{8,10},{9,11},{10,... | collective-permute-start | bytes 92168 | tf_op jit(solution)/shard_map/ppermute | solution.py:25
  78.7 19.4 %collective-permute-start.19 = (bf16[96,640]{1,0:T(8,128)(2,1)S(1)}, bf16[96,640]{1,0:T(8,128)(2,1)S(1)}, u32[]{:S(2)}, u32[]{:S(2)}) collective-permute-start(bf16[96,640]{1,0:T(8,128)(2,1)S(1)} %bitcast.25), channel_id=1, source_target_pairs={{0,24},{4,28},{8,16},{12,20},{16,8},{20,12},{24,0},{28,4},{1,25},{... | collective-permute-start | bytes 368648 | tf_op jit(solution)/shard_map/ppermute | solution.py:25
  80.5 5.8 %collective-permute-start.27 = (bf16[24,640]{1,0:T(8,128)(2,1)S(1)}, bf16[24,640]{1,0:T(8,128)(2,1)S(1)}, u32[]{:S(2)}, u32[]{:S(2)}) collective-permute-start(bf16[24,640]{1,0:T(8,128)(2,1)S(1)} %get-tuple-element.88), channel_id=1, source_target_pairs={{0,3},{1,2},{2,1},{3,0},{4,7},{5,6},{6,5},{7,4},{8,11},{9,10},{10,... | collective-permute-start | bytes 92168 | tf_op jit(solution)/shard_map/ppermute | solution.py:25
  82.1 4.9 %collective-permute-start.28 = (bf16[24,640]{1,0:T(8,128)(2,1)S(1)}, bf16[24,640]{1,0:T(8,128)(2,1)S(1)}, u32[]{:S(2)}, u32[]{:S(2)}) collective-permute-start(bf16[24,640]{1,0:T(8,128)(2,1)S(1)} %get-tuple-element.89), channel_id=1, source_target_pairs={{0,1},{1,0},{2,3},{3,2},{4,5},{5,4},{6,7},{7,6},{8,9},{9,8},{10,11... | collective-permute-start | bytes 92168 | tf_op jit(solution)/shard_map/ppermute | solution.py:25
  82.1 4.9 %collective-permute-start.29 = (bf16[24,640]{1,0:T(8,128)(2,1)S(1)}, bf16[24,640]{1,0:T(8,128)(2,1)S(1)}, u32[]{:S(2)}, u32[]{:S(2)}) collective-permute-start(bf16[24,640]{1,0:T(8,128)(2,1)S(1)} %get-tuple-element.90), channel_id=1, source_target_pairs={{0,2},{1,3},{2,0},{3,1},{4,6},{5,7},{6,4},{7,5},{8,10},{9,11},{10,... | collective-permute-start | bytes 92168 | tf_op jit(solution)/shard_map/ppermute | solution.py:25
  87.1 5.8 %collective-permute-start.30 = (bf16[24,640]{1,0:T(8,128)(2,1)S(1)}, bf16[24,640]{1,0:T(8,128)(2,1)S(1)}, u32[]{:S(2)}, u32[]{:S(2)}) collective-permute-start(bf16[24,640]{1,0:T(8,128)(2,1)S(1)} %shard_map.142.own_ref), channel_id=1, source_target_pairs={{0,3},{1,2},{2,1},{3,0},{4,7},{5,6},{6,5},{7,4},{8,11},{9,10},{10,... | collective-permute-start | bytes 92168 | tf_op jit(solution)/shard_map/ppermute | solution.py:25
  89.4 4.6 %collective-permute-start.31 = (bf16[24,640]{1,0:T(8,128)(2,1)S(1)}, bf16[24,640]{1,0:T(8,128)(2,1)S(1)}, u32[]{:S(2)}, u32[]{:S(2)}) collective-permute-start(bf16[24,640]{1,0:T(8,128)(2,1)S(1)} %shard_map.142.own_ref), channel_id=1, source_target_pairs={{0,1},{1,0},{2,3},{3,2},{4,5},{5,4},{6,7},{7,6},{8,9},{9,8},{10,11... | collective-permute-start | bytes 92168 | tf_op jit(solution)/shard_map/ppermute | solution.py:25
  90.4 4.8 %collective-permute-start.32 = (bf16[24,640]{1,0:T(8,128)(2,1)S(1)}, bf16[24,640]{1,0:T(8,128)(2,1)S(1)}, u32[]{:S(2)}, u32[]{:S(2)}) collective-permute-start(bf16[24,640]{1,0:T(8,128)(2,1)S(1)} %shard_map.142.own_ref), channel_id=1, source_target_pairs={{0,2},{1,3},{2,0},{3,1},{4,6},{5,7},{6,4},{7,5},{8,10},{9,11},{10,... | collective-permute-start | bytes 92168 | tf_op jit(solution)/shard_map/ppermute | solution.py:25
  91.5 7.2 %collective-permute-start.20 = (bf16[96,640]{1,0:T(8,128)(2,1)S(1)}, bf16[96,640]{1,0:T(8,128)(2,1)S(1)}, u32[]{:S(2)}, u32[]{:S(2)}) collective-permute-start(bf16[96,640]{1,0:T(8,128)(2,1)S(1)} %bitcast.26), channel_id=1, source_target_pairs={{0,8},{4,12},{8,0},{12,4},{16,24},{20,28},{24,16},{28,20},{1,9},{5... | collective-permute-start | bytes 368648 | tf_op jit(solution)/shard_map/ppermute | solution.py:25
  92.8 5.9 %collective-permute-start.21 = (bf16[96,640]{1,0:T(8,128)(2,1)S(1)}, bf16[96,640]{1,0:T(8,128)(2,1)S(1)}, u32[]{:S(2)}, u32[]{:S(2)}) collective-permute-start(bf16[96,640]{1,0:T(8,128)(2,1)S(1)} %bitcast.27), channel_id=1, source_target_pairs={{0,16},{4,20},{8,24},{12,28},{16,0},{20,4},{24,8},{28,12},{1,17},{... | collective-permute-start | bytes 368648 | tf_op jit(solution)/shard_map/ppermute | solution.py:25
  95.2 5.8 %collective-permute-start.33 = (bf16[96,640]{1,0:T(8,128)(2,1)S(1)}, bf16[96,640]{1,0:T(8,128)(2,1)S(1)}, u32[]{:S(2)}, u32[]{:S(2)}) collective-permute-start(bf16[96,640]{1,0:T(8,128)(2,1)S(1)} %bitcast.29), channel_id=1, source_target_pairs={{0,24},{4,28},{8,16},{12,20},{16,8},{20,12},{24,0},{28,4},{1,25},{... | collective-permute-start | bytes 368648 | tf_op jit(solution)/shard_map/ppermute | solution.py:25
  96.6 5.7 %collective-permute-start.34 = (bf16[96,640]{1,0:T(8,128)(2,1)S(1)}, bf16[96,640]{1,0:T(8,128)(2,1)S(1)}, u32[]{:S(2)}, u32[]{:S(2)}) collective-permute-start(bf16[96,640]{1,0:T(8,128)(2,1)S(1)} %bitcast.30), channel_id=1, source_target_pairs={{0,8},{4,12},{8,0},{12,4},{16,24},{20,28},{24,16},{28,20},{1,9},{5... | collective-permute-start | bytes 368648 | tf_op jit(solution)/shard_map/ppermute | solution.py:25
  98.0 4.9 %collective-permute-start.35 = (bf16[96,640]{1,0:T(8,128)(2,1)S(1)}, bf16[96,640]{1,0:T(8,128)(2,1)S(1)}, u32[]{:S(2)}, u32[]{:S(2)}) collective-permute-start(bf16[96,640]{1,0:T(8,128)(2,1)S(1)} %bitcast.31), channel_id=1, source_target_pairs={{0,16},{4,20},{8,24},{12,28},{16,0},{20,4},{24,8},{28,12},{1,17},{... | collective-permute-start | bytes 368648 | tf_op jit(solution)/shard_map/ppermute | solution.py:25
  98.8 4.4 %collective-permute-start.22 = (bf16[384,640]{1,0:T(8,128)(2,1)S(1)}, bf16[384,640]{1,0:T(8,128)(2,1)S(1)}, u32[]{:S(2)}, u32[]{:S(2)}) collective-permute-start(bf16[384,640]{1,0:T(8,128)(2,1)S(1)} %bitcast.17), channel_id=1, source_target_pairs={{0,4},{4,0},{8,12},{12,8},{16,20},{20,16},{24,28},{28,24},{1,5},{5... | collective-permute-start | bytes 1474568 | tf_op jit(solution)/shard_map/ppermute | solution.py:25
  103.0 2.9 %collective-permute-start.36 = (bf16[384,640]{1,0:T(8,128)(2,1)S(1)}, bf16[384,640]{1,0:T(8,128)(2,1)S(1)}, u32[]{:S(2)}, u32[]{:S(2)}) collective-permute-start(bf16[384,640]{1,0:T(8,128)(2,1)S(1)} %bitcast.20), channel_id=1, source_target_pairs={{0,4},{4,0},{8,12},{12,8},{16,20},{20,16},{24,28},{28,24},{1,5},{5... | collective-permute-start | bytes 1474568 | tf_op jit(solution)/shard_map/ppermute | solution.py:25

commit v2 on v1

--- a/solution.py
+++ b/solution.py
@@ -31,7 +31,7 @@
 
 
 def order(size):
-    return sorted(range(1, size), key=lambda k: -bin(k).count("1"))
+    return list(range(size - 1, 0, -1))
 
 
 def place_on(stage):
@@ -594,7 +594,7 @@
         functools.partial(score_kernel, members, bands, count),
         [
             shape((half, lanes)),
-            shape((half, lanes)),
+            shape((half, lanes), BF),
             shape((cells, channels)),
             shape((cells, hidden_units), BF),
         ],
@@ -621,7 +621,7 @@
     first = across_plane(*one)
     own, sent = call(
         rest_kernel,
-        [shape((half, lanes)), shape((half, lanes))],
+        [shape((half, lanes)), shape((half, lanes), BF)],
         (
             d_preact, turned, scaled, window, wide, gain_row,
             one[0],

time: 109 us -> 107 us (0.982)
  waiting for transfers between devices: 40.5 us -> 36.6 us
  starting transfers between devices: 40.5 us -> 42.2 us
    ppermute x35, waiting for transfers between devices: 28 us -> 24.1 us  [swap(): return lax.ppermute(value, axis, [(i, i ^ mask) for i in range(count)])]
    ppermute x35, starting transfers between devices: 36.7 us -> 38.4 us  [swap(): return lax.ppermute(value, axis, [(i, i ^ mask) for i in range(count)])]
  transfers between devices with their start and end apart: 37 -> 37, of which waited for: 19 -> 17; matrix products, arithmetic and copies ran while one was open for 0% -> 0% of each run, Pallas kernels for 6% -> 7%
where the time goes in v2:
time: 107 us; the launch traced here: 106 us
  starting transfers between devices  42.2 us (39%)
  waiting for transfers between devices  36.6 us (34%)
  Pallas kernels  21 us (20%)
  local copies, waits for them, and re-layouts  5.54 us (5%)
    ppermute x35, starting transfers between devices, swap(): return lax.ppermute(value, axis, [(i, i ^ mask) for i in range(count)])  38.4 us
    ppermute x35, waiting for transfers between devices, swap(): return lax.ppermute(value, axis, [(i, i ^ mask) for i in range(count)])  24.1 us
    pallas_call x19, Pallas kernels, call(): pl.pallas_call(kernel, out_shape=outs, in_specs=[spec] * len(args), out_s...  21 us
    ppermute x2, waiting for transfers between devices, trade(): return lax.ppermute(value, 'lat', pairs + [(j, i) for i, j in pairs])  12.5 us
    unnamed x19, local copies, waits for them, and re-layouts  5.54 us
    ppermute x2, starting transfers between devices, trade(): return lax.ppermute(value, 'lat', pairs + [(j, i) for i, j in pairs])  3.79 us
  transfers between devices with their start and end apart: 37, of which 17 were waited for; matrix products, arithmetic and copies ran while one was open for 0% of the time, Pallas kernels for 7%

profile of v2, /device:TPU:0, one launch (start us, length us, event | category | flops | bytes accessed | tf_op | source)
XLA Modules:
  0.0 106.2 jit_solution(10696093405464901901)
XLA Ops:
  0.7 1.3 %copy-done.1 = f32[1,641,2,160]{1,3,2,0:T(8,128)S(1)} copy-done((f32[1,641,2,160]{1,3,2,0:T(8,128)S(1)}, f32[1,641,2,160]{1,3,2,0:T(8,128)}, u32[]{:S(2)}) %copy-start.1) | copy-done | bytes 820504
  2.0 0.2 shard_map.128
  2.1 3.1 %collective-permute-start = (f32[328,640]{1,0:T(8,128)S(1)}, f32[328,640]{1,0:T(8,128)S(1)}, u32[]{:S(2)}, u32[]{:S(2)}) collective-permute-start(f32[328,640]{1,0:T(8,128)S(1)} %shard_map.128), channel_id=1, source_target_pairs={{0,1},{2,3},{1,0},{3,2},{4,5},{6,7},{5,4},{7,6},{8,9},{10,11},{9,8... | collective-permute-start | bytes 2519048 | tf_op jit(solution)/shard_map/ppermute | solution.py:539
  5.2 0.7 collective-permute-start.1
  6.0 0.9 copy-done.3
  6.8 0.9 copy-done.5
  7.7 0.9 copy-done.6
  8.6 0.7 copy-done.7
  9.3 0.7 copy-done.8
  10.0 1.4 %shard_map.127 = (f32[320,641]{1,0:T(8,128)S(1)}, f32[1,641]{1,0:T(1,128)S(1)}, f32[72,320]{1,0:T(8,128)S(1)}, f32[72,320]{1,0:T(8,128)S(1)}) custom-call(f32[2,160,641]{2,1,0:T(8,128)S(1)} %bitcast.13, f32[25,641]{1,0:T(8,128)S(1)} %copy-done.5, f32[641]{0:T(1024)S(1)} %copy-done.7, f32[72,2,160]{2,1,0:T(2,128)S(1)} %copy-done.6, f32[72]{0:T(128)S(1)} %copy-done.8, ...), custom_call_target="tpu_custom_call" | custom-call | flops 100000000 | bytes 3722784 | tf_op jit(solution)/shard_map/pallas_call | solution.py:125
  11.4 12.5 %collective-permute-done.first_ref = f32[328,640]{1,0:T(8,128)S(1)} collective-permute-done((f32[328,640]{1,0:T(8,128)S(1)}, f32[328,640]{1,0:T(8,128)S(1)}, u32[]{:S(2)}, u32[]{:S(2)}) %collective-permute-start) | collective-permute-done | bytes 839712 | tf_op jit(solution)/shard_map/ppermute | solution.py:539
  23.9 5.0 %shard_map.129 = (f32[72,320]{1,0:T(8,128)S(1)}, f32[72,320]{1,0:T(8,128)S(1)}, f32[6,176,641]{2,1,0:T(8,128)S(1)}, f32[320,641]{1,0:T(8,128)S(1)}, f32[320,1]{1...) custom-call(f32[2,160,641]{2,1,0:T(8,128)S(1)} %bitcast.14, ...), custom_call_target="tpu_custom_call" | custom-call | flops 1051855360 | bytes 13854080 | tf_op jit(solution)/shard_map/pallas_call | solution.py:125
  29.0 2.7 %collective-permute-start.2 = (f32[72,320]{1,0:T(8,128)S(1)}, f32[72,320]{1,0:T(8,128)S(1)}, u32[]{:S(2)}, u32[]{:S(2)}) collective-permute-start(f32[72,320]{1,0:T(8,128)S(1)} %get-tuple-element.54.refs_7_), channel_id=1, source_target_pairs={{0,24},{4,28},{8,16},{12,20},{16,8},{20,12},{24,0},{28,4},{1,25},{... | collective-permute-start | bytes 276488 | tf_op jit(solution)/shard_map/ppermute | solution.py:25
  31.6 0.5 collective-permute-start.3
  32.1 0.4 collective-permute-start.4
  32.5 2.7 %collective-permute-done.2.refs_0_ = f32[72,320]{1,0:T(8,128)S(1)} collective-permute-done((f32[72,320]{1,0:T(8,128)S(1)}, f32[72,320]{1,0:T(8,128)S(1)}, u32[]{:S(2)}, u32[]{:S(2)}) %collective-permute-start.2) | collective-permute-done | bytes 92192 | tf_op jit(solution)/shard_map/ppermute | solution.py:25
  35.2 1.3 %collective-permute-done.3.refs_1_ = f32[72,320]{1,0:T(8,128)S(1)} collective-permute-done((f32[72,320]{1,0:T(8,128)S(1)}, f32[72,320]{1,0:T(8,128)S(1)}, u32[]{:S(2)}, u32[]{:S(2)}) %collective-permute-start.3) | collective-permute-done | bytes 92192 | tf_op jit(solution)/shard_map/ppermute | solution.py:25
  36.5 0.4 collective-permute-done.4.refs_2_
  36.9 0.1 collective-permute-start.8
  37.0 1.1 %shard_map.130 = (f32[320,1282]{1,0:T(8,128)S(1)}, bf16[641,320]{1,0:T(8,128)(2,1)S(1)}) custom-call(f32[320,1282]{1,0:T(8,128)S(1)} %get-tuple-element.59.preact_ref, bf16[320,641]{1,0:T(8,128)(2,1)S(1)} %get-tuple-element.60.scaled_ref), custom_call_target="tpu_custom_call" | custom-call | flops 525927680 | bytes 4102400 | tf_op jit(solution)/shard_map/pallas_call | solution.py:125
  38.2 2.2 %shard_map.131 = (f32[384,640]{1,0:T(8,128)S(1)}, bf16[384,640]{1,0:T(8,128)(2,1)S(1)}, f32[320,641]{1,0:T(8,128)S(1)}, bf16[320,1282]{1,0:T(8,128)(2,1)S(1)}) custom-call(f32[72,320]{1,0:T(8,128)S(1)} %collective-permute-done.2.refs_0_, f32[72,320]{1,0:T(8,128)S(1)} %collective-permute-done.3.refs_1_, f32[72,320]{1,0:T(8,128)S(1)} %collective-permute-done.4.refs_2_, ...), custom_call_target="tpu_custom_call" | custom-call | flops 1051855360 | bytes 9054868 | tf_op jit(solution)/shard_map/pallas_call | solution.py:125
  40.4 0.4 collective-permute-start.9
  40.9 1.3 %shard_map.138 = (f32[320,641]{1,0:T(8,128)S(1)}, f32[1,641]{1,0:T(1,128)S(1)}) custom-call(bf16[320,1282]{1,0:T(8,128)(2,1)S(1)} %get-tuple-element.74.preact_ref, bf16[641,1282]{1,0:T(8,128)(2,1)S(1)} %copy-done, f32[1,641]{1,0:T(1,128)S(1)} %get-tuple-element.52.gain_ref, f32[320,641]{1,0:T(8,128)S(1)} %get-tuple-element.76.normed_ref, ...), custom_call_target="tpu_custom_call" | custom-call | flops 525927680 | bytes 4931852 | tf_op jit(solution)/shard_map/pallas_call | solution.py:125
  42.2 0.2 collective-permute-done.9.refs_1_
  42.4 0.2 shard_map.132
  42.5 3.9 %shard_map.139 = (f32[384,640]{1,0:T(8,128)S(1)}, bf16[384,640]{1,0:T(8,128)(2,1)S(1)}) custom-call(bf16[320,1282]{1,0:T(8,128)(2,1)S(1)} %get-tuple-element.74.preact_ref, bf16[641,320]{1,0:T(8,128)(2,1)S(1)} %get-tuple-element.62.refs_15_.turned_ref, bf16[320,641]{1,0:T(8,128)(2,1)S(1)} %get-tuple-element.60.scaled_ref, ...), custom_call_target="tpu_custom_call" | custom-call | flops 1051855360 | bytes 6891908 | tf_op jit(solution)/shard_map/pallas_call | solution.py:125
  46.5 0.4 collective-permute-start.23
  46.9 1.5 %collective-permute-start.10 = (bf16[96,640]{1,0:T(8,128)(2,1)S(1)}, bf16[96,640]{1,0:T(8,128)(2,1)S(1)}, u32[]{:S(2)}, u32[]{:S(2)}) collective-permute-start(bf16[96,640]{1,0:T(8,128)(2,1)S(1)} %get-tuple-element.66), channel_id=1, source_target_pairs={{0,24},{4,28},{8,16},{12,20},{16,8},{20,12},{24,0},{28,4},{1,25},{... | collective-permute-start | bytes 368648 | tf_op jit(solution)/shard_map/ppermute | solution.py:25
  48.5 1.1 %collective-permute-start.11 = (bf16[96,640]{1,0:T(8,128)(2,1)S(1)}, bf16[96,640]{1,0:T(8,128)(2,1)S(1)}, u32[]{:S(2)}, u32[]{:S(2)}) collective-permute-start(bf16[96,640]{1,0:T(8,128)(2,1)S(1)} %get-tuple-element.67), channel_id=1, source_target_pairs={{0,16},{4,20},{8,24},{12,28},{16,0},{20,4},{24,8},{28,12},{1,17},{... | collective-permute-start | bytes 368648 | tf_op jit(solution)/shard_map/ppermute | solution.py:25
  49.6 0.9 collective-permute-start.12
  50.4 3.6 %collective-permute-done.10.refs_1_ = bf16[96,640]{1,0:T(8,128)(2,1)S(1)} collective-permute-done((bf16[96,640]{1,0:T(8,128)(2,1)S(1)}, bf16[96,640]{1,0:T(8,128)(2,1)S(1)}, u32[]{:S(2)}, u32[]{:S(2)}) %collective-permute-start.10) | collective-permute-done | bytes 122912 | tf_op jit(solution)/shard_map/ppermute | solution.py:25
  54.0 1.8 %collective-permute-done.11.refs_2_ = bf16[96,640]{1,0:T(8,128)(2,1)S(1)} collective-permute-done((bf16[96,640]{1,0:T(8,128)(2,1)S(1)}, bf16[96,640]{1,0:T(8,128)(2,1)S(1)}, u32[]{:S(2)}, u32[]{:S(2)}) %collective-permute-start.11) | collective-permute-done | bytes 122912 | tf_op jit(solution)/shard_map/ppermute | solution.py:25
  56.0 3.7 %collective-permute-start.13 = (bf16[24,640]{1,0:T(8,128)(2,1)S(1)}, bf16[24,640]{1,0:T(8,128)(2,1)S(1)}, u32[]{:S(2)}, u32[]{:S(2)}) collective-permute-start(bf16[24,640]{1,0:T(8,128)(2,1)S(1)} %get-tuple-element.70), channel_id=1, source_target_pairs={{0,3},{1,2},{2,1},{3,0},{4,7},{5,6},{6,5},{7,4},{8,11},{9,10},{10,... | collective-permute-start | bytes 92168 | tf_op jit(solution)/shard_map/ppermute | solution.py:25
  59.7 2.5 %collective-permute-start.14 = (bf16[24,640]{1,0:T(8,128)(2,1)S(1)}, bf16[24,640]{1,0:T(8,128)(2,1)S(1)}, u32[]{:S(2)}, u32[]{:S(2)}) collective-permute-start(bf16[24,640]{1,0:T(8,128)(2,1)S(1)} %get-tuple-element.71), channel_id=1, source_target_pairs={{0,2},{1,3},{2,0},{3,1},{4,6},{5,7},{6,4},{7,5},{8,10},{9,11},{10,... | collective-permute-start | bytes 92168 | tf_op jit(solution)/shard_map/ppermute | solution.py:25
  62.1 0.4 collective-permute-start.15
  62.5 0.2 shard_map.140
  62.7 1.4 %collective-permute-start.24 = (bf16[96,640]{1,0:T(8,128)(2,1)S(1)}, bf16[96,640]{1,0:T(8,128)(2,1)S(1)}, u32[]{:S(2)}, u32[]{:S(2)}) collective-permute-start(bf16[96,640]{1,0:T(8,128)(2,1)S(1)} %get-tuple-element.84), channel_id=1, source_target_pairs={{0,24},{4,28},{8,16},{12,20},{16,8},{20,12},{24,0},{28,4},{1,25},{... | collective-permute-start | bytes 368648 | tf_op jit(solution)/shard_map/ppermute | solution.py:25
  64.1 1.2 %collective-permute-start.25 = (bf16[96,640]{1,0:T(8,128)(2,1)S(1)}, bf16[96,640]{1,0:T(8,128)(2,1)S(1)}, u32[]{:S(2)}, u32[]{:S(2)}) collective-permute-start(bf16[96,640]{1,0:T(8,128)(2,1)S(1)} %get-tuple-element.85), channel_id=1, source_target_pairs={{0,16},{4,20},{8,24},{12,28},{16,0},{20,4},{24,8},{28,12},{1,17},{... | collective-permute-start | bytes 368648 | tf_op jit(solution)/shard_map/ppermute | solution.py:25
  65.3 0.9 collective-permute-start.26
  66.3 2.6 %collective-permute-start.16 = (bf16[24,640]{1,0:T(8,128)(2,1)S(1)}, bf16[24,640]{1,0:T(8,128)(2,1)S(1)}, u32[]{:S(2)}, u32[]{:S(2)}) collective-permute-start(bf16[24,640]{1,0:T(8,128)(2,1)S(1)} %shard_map.134.own_ref), channel_id=1, source_target_pairs={{0,3},{1,2},{2,1},{3,0},{4,7},{5,6},{6,5},{7,4},{8,11},{9,10},{10,... | collective-permute-start | bytes 92168 | tf_op jit(solution)/shard_map/ppermute | solution.py:25
  68.8 0.6 collective-permute-start.17
  69.5 2.6 %collective-permute-done.16.refs_0_ = bf16[24,640]{1,0:T(8,128)(2,1)S(1)} collective-permute-done((bf16[24,640]{1,0:T(8,128)(2,1)S(1)}, bf16[24,640]{1,0:T(8,128)(2,1)S(1)}, u32[]{:S(2)}, u32[]{:S(2)}) %collective-permute-start.16) | collective-permute-done | bytes 30752 | tf_op jit(solution)/shard_map/ppermute | solution.py:25
  72.1 0.2 collective-permute-start.18
  72.3 1.3 %collective-permute-done.17.refs_1_ = bf16[24,640]{1,0:T(8,128)(2,1)S(1)} collective-permute-done((bf16[24,640]{1,0:T(8,128)(2,1)S(1)}, bf16[24,640]{1,0:T(8,128)(2,1)S(1)}, u32[]{:S(2)}, u32[]{:S(2)}) %collective-permute-start.17) | collective-permute-done | bytes 30752 | tf_op jit(solution)/shard_map/ppermute | solution.py:25
  73.6 2.4 %collective-permute-done.18.refs_2_ = bf16[24,640]{1,0:T(8,128)(2,1)S(1)} collective-permute-done((bf16[24,640]{1,0:T(8,128)(2,1)S(1)}, bf16[24,640]{1,0:T(8,128)(2,1)S(1)}, u32[]{:S(2)}, u32[]{:S(2)}) %collective-permute-start.18) | collective-permute-done | bytes 30752 | tf_op jit(solution)/shard_map/ppermute | solution.py:25
  76.0 1.4 %collective-permute-start.19 = (bf16[96,640]{1,0:T(8,128)(2,1)S(1)}, bf16[96,640]{1,0:T(8,128)(2,1)S(1)}, u32[]{:S(2)}, u32[]{:S(2)}) collective-permute-start(bf16[96,640]{1,0:T(8,128)(2,1)S(1)} %bitcast.25), channel_id=1, source_target_pairs={{0,24},{4,28},{8,16},{12,20},{16,8},{20,12},{24,0},{28,4},{1,25},{... | collective-permute-start | bytes 368648 | tf_op jit(solution)/shard_map/ppermute | solution.py:25
  77.5 2.9 %collective-permute-start.27 = (bf16[24,640]{1,0:T(8,128)(2,1)S(1)}, bf16[24,640]{1,0:T(8,128)(2,1)S(1)}, u32[]{:S(2)}, u32[]{:S(2)}) collective-permute-start(bf16[24,640]{1,0:T(8,128)(2,1)S(1)} %get-tuple-element.88), channel_id=1, source_target_pairs={{0,3},{1,2},{2,1},{3,0},{4,7},{5,6},{6,5},{7,4},{8,11},{9,10},{10,... | collective-permute-start | bytes 92168 | tf_op jit(solution)/shard_map/ppermute | solution.py:25
  80.4 1.5 %collective-permute-start.29 = (bf16[24,640]{1,0:T(8,128)(2,1)S(1)}, bf16[24,640]{1,0:T(8,128)(2,1)S(1)}, u32[]{:S(2)}, u32[]{:S(2)}) collective-permute-start(bf16[24,640]{1,0:T(8,128)(2,1)S(1)} %get-tuple-element.90), channel_id=1, source_target_pairs={{0,1},{1,0},{2,3},{3,2},{4,5},{5,4},{6,7},{7,6},{8,9},{9,8},{10,11... | collective-permute-start | bytes 92168 | tf_op jit(solution)/shard_map/ppermute | solution.py:25
  82.0 1.3 %collective-permute-done.27.refs_1_ = bf16[24,640]{1,0:T(8,128)(2,1)S(1)} collective-permute-done((bf16[24,640]{1,0:T(8,128)(2,1)S(1)}, bf16[24,640]{1,0:T(8,128)(2,1)S(1)}, u32[]{:S(2)}, u32[]{:S(2)}) %collective-permute-start.27) | collective-permute-done | bytes 30752 | tf_op jit(solution)/shard_map/ppermute | solution.py:25
  83.3 2.6 %collective-permute-done.28.refs_2_ = bf16[24,640]{1,0:T(8,128)(2,1)S(1)} collective-permute-done((bf16[24,640]{1,0:T(8,128)(2,1)S(1)}, bf16[24,640]{1,0:T(8,128)(2,1)S(1)}, u32[]{:S(2)}, u32[]{:S(2)}) %collective-permute-start.28) | collective-permute-done | bytes 30752 | tf_op jit(solution)/shard_map/ppermute | solution.py:25
  86.0 2.1 %collective-permute-start.30 = (bf16[24,640]{1,0:T(8,128)(2,1)S(1)}, bf16[24,640]{1,0:T(8,128)(2,1)S(1)}, u32[]{:S(2)}, u32[]{:S(2)}) collective-permute-start(bf16[24,640]{1,0:T(8,128)(2,1)S(1)} %shard_map.142.own_ref), channel_id=1, source_target_pairs={{0,3},{1,2},{2,1},{3,0},{4,7},{5,6},{6,5},{7,4},{8,11},{9,10},{10,... | collective-permute-start | bytes 92168 | tf_op jit(solution)/shard_map/ppermute | solution.py:25
  88.0 2.4 %collective-permute-start.32 = (bf16[24,640]{1,0:T(8,128)(2,1)S(1)}, bf16[24,640]{1,0:T(8,128)(2,1)S(1)}, u32[]{:S(2)}, u32[]{:S(2)}) collective-permute-start(bf16[24,640]{1,0:T(8,128)(2,1)S(1)} %shard_map.142.own_ref), channel_id=1, source_target_pairs={{0,1},{1,0},{2,3},{3,2},{4,5},{5,4},{6,7},{7,6},{8,9},{9,8},{10,11... | collective-permute-start | bytes 92168 | tf_op jit(solution)/shard_map/ppermute | solution.py:25
  90.4 1.2 %collective-permute-start.20 = (bf16[96,640]{1,0:T(8,128)(2,1)S(1)}, bf16[96,640]{1,0:T(8,128)(2,1)S(1)}, u32[]{:S(2)}, u32[]{:S(2)}) collective-permute-start(bf16[96,640]{1,0:T(8,128)(2,1)S(1)} %bitcast.26), channel_id=1, source_target_pairs={{0,16},{4,20},{8,24},{12,28},{16,0},{20,4},{24,8},{28,12},{1,17},{... | collective-permute-start | bytes 368648 | tf_op jit(solution)/shard_map/ppermute | solution.py:25
  91.6 0.1 collective-permute-done.30.refs_0_
  91.7 1.7 %collective-permute-start.21 = (bf16[96,640]{1,0:T(8,128)(2,1)S(1)}, bf16[96,640]{1,0:T(8,128)(2,1)S(1)}, u32[]{:S(2)}, u32[]{:S(2)}) collective-permute-start(bf16[96,640]{1,0:T(8,128)(2,1)S(1)} %bitcast.27), channel_id=1, source_target_pairs={{0,8},{4,12},{8,0},{12,4},{16,24},{20,28},{24,16},{28,20},{1,9},{5... | collective-permute-start | bytes 368648 | tf_op jit(solution)/shard_map/ppermute | solution.py:25
  93.4 1.1 %collective-permute-start.33 = (bf16[96,640]{1,0:T(8,128)(2,1)S(1)}, bf16[96,640]{1,0:T(8,128)(2,1)S(1)}, u32[]{:S(2)}, u32[]{:S(2)}) collective-permute-start(bf16[96,640]{1,0:T(8,128)(2,1)S(1)} %bitcast.29), channel_id=1, source_target_pairs={{0,24},{4,28},{8,16},{12,20},{16,8},{20,12},{24,0},{28,4},{1,25},{... | collective-permute-start | bytes 368648 | tf_op jit(solution)/shard_map/ppermute | solution.py:25
  94.5 1.4 %collective-permute-start.34 = (bf16[96,640]{1,0:T(8,128)(2,1)S(1)}, bf16[96,640]{1,0:T(8,128)(2,1)S(1)}, u32[]{:S(2)}, u32[]{:S(2)}) collective-permute-start(bf16[96,640]{1,0:T(8,128)(2,1)S(1)} %bitcast.30), channel_id=1, source_target_pairs={{0,16},{4,20},{8,24},{12,28},{16,0},{20,4},{24,8},{28,12},{1,17},{... | collective-permute-start | bytes 368648 | tf_op jit(solution)/shard_map/ppermute | solution.py:25
  95.9 1.1 %collective-permute-start.35 = (bf16[96,640]{1,0:T(8,128)(2,1)S(1)}, bf16[96,640]{1,0:T(8,128)(2,1)S(1)}, u32[]{:S(2)}, u32[]{:S(2)}) collective-permute-start(bf16[96,640]{1,0:T(8,128)(2,1)S(1)} %bitcast.31), channel_id=1, source_target_pairs={{0,8},{4,12},{8,0},{12,4},{16,24},{20,28},{24,16},{28,20},{1,9},{5... | collective-permute-start | bytes 368648 | tf_op jit(solution)/shard_map/ppermute | solution.py:25
  97.2 2.2 %collective-permute-done.33.refs_0_ = bf16[96,640]{1,0:T(8,128)(2,1)S(1)} collective-permute-done((bf16[96,640]{1,0:T(8,128)(2,1)S(1)}, bf16[96,640]{1,0:T(8,128)(2,1)S(1)}, u32[]{:S(2)}, u32[]{:S(2)}) %collective-permute-start.33) | collective-permute-done | bytes 122912 | tf_op jit(solution)/shard_map/ppermute | solution.py:25
  99.4 1.2 %collective-permute-done.34.refs_1_ = bf16[96,640]{1,0:T(8,128)(2,1)S(1)} collective-permute-done((bf16[96,640]{1,0:T(8,128)(2,1)S(1)}, bf16[96,640]{1,0:T(8,128)(2,1)S(1)}, u32[]{:S(2)}, u32[]{:S(2)}) %collective-permute-start.34) | collective-permute-done | bytes 122912 | tf_op jit(solution)/shard_map/ppermute | solution.py:25
  100.6 0.1 collective-permute-done.35.refs_2_
  100.9 0.2 copy.14.head_ref
  101.1 2.7 %shard_map.137 = (f32[1,1]{1,0:T(1,128)}, f32[641,1282]{1,0:T(8,128)}, f32[72,641]{1,0:T(8,128)}) custom-call(bf16[384,640]{1,0:T(8,128)(2,1)S(1)} %bitcast.18, bf16[384,640]{1,0:T(8,128)(2,1)S(1)} %collective-permute-done.22.got_ref.got_one_ref, bf16[641,72]{1,0:T(8,128)(2,1)S(1)} %copy.14.head_ref), custom_call_target="tpu_custom_call" | custom-call | flops 131481920 | bytes 4547004 | tf_op jit(solution)/shard_map/pallas_call | solution.py:125
  103.7 2.5 %shard_map.145 = (f32[25,641]{1,0:T(8,128)}, f32[641]{0:T(1024)}, f32[641,1282]{1,0:T(8,128)}) custom-call(bf16[384,640]{1,0:T(8,128)(2,1)S(1)} %bitcast.19, bf16[384,640]{1,0:T(8,128)(2,1)S(1)} %collective-permute-done.22.got_ref.got_one_ref, bf16[384,640]{1,0:T(8,128)(2,1)S(1)} %bitcast.21, bf16[384,640]{1,0:T(8,128)(2,1)S(1)} %collective-permute-done.36.got_two_ref), custom_call_target="tpu_custom_call" | custom-call | flops 131481920 | bytes 5319792 | tf_op jit(solution)/shard_map/pallas_call | solution.py:125
  (48 shorter events, 0.7 us)
Async XLA Ops:
  0.6 5.3 %copy-start = (bf16[641,1282]{1,0:T(8,128)(2,1)S(1)}, bf16[641,1282]{1,0:T(8,128)(2,1)}, u32[]{:S(2)}) copy-start(bf16[641,1282]{1,0:T(8,128)(2,1)} %up_ref.3) | copy-start | bytes 4930576
  0.6 1.3 %copy-start.1 = (f32[1,641,2,160]{1,3,2,0:T(8,128)S(1)}, f32[1,641,2,160]{1,3,2,0:T(8,128)}, u32[]{:S(2)}) copy-start(f32[1,641,2,160]{1,3,2,0:T(8,128)} %param.8) | copy-start | bytes 2461444
  2.1 21.8 %copy-start.2 = (bf16[1282,641]{0,1:T(8,128)(2,1)S(1)}, bf16[1282,641]{0,1:T(8,128)(2,1)}, u32[]{:S(2)}) copy-start(bf16[1282,641]{0,1:T(8,128)(2,1)} %param.12) | copy-start | bytes 4930576
  2.1 21.8 %collective-permute-start = (f32[328,640]{1,0:T(8,128)S(1)}, f32[328,640]{1,0:T(8,128)S(1)}, u32[]{:S(2)}, u32[]{:S(2)}) collective-permute-start(f32[328,640]{1,0:T(8,128)S(1)} %shard_map.128), channel_id=1, source_target_pairs={{0,1},{2,3},{1,0},{3,2},{4,5},{6,7},{5,4},{7,6},{8,9},{10,11},{9,8... | collective-permute-start | bytes 2519048 | tf_op jit(solution)/shard_map/ppermute | solution.py:539
  5.2 18.7 %collective-permute-start.1 = (f32[328,640]{1,0:T(8,128)S(1)}, f32[328,640]{1,0:T(8,128)S(1)}, u32[]{:S(2)}, u32[]{:S(2)}) collective-permute-start(f32[328,640]{1,0:T(8,128)S(1)} %shard_map.128), channel_id=1, source_target_pairs={{1,2},{2,1},{5,6},{6,5},{9,10},{10,9},{13,14},{14,13},{17,18},{18,... | collective-permute-start | bytes 2519048 | tf_op jit(solution)/shard_map/ppermute | solution.py:539
  5.9 0.9 copy-start.3
  6.8 0.9 copy-start.5
  7.7 0.9 copy-start.6
  8.6 0.7 copy-start.7
  9.3 0.7 copy-start.8
  29.0 6.3 %collective-permute-start.2 = (f32[72,320]{1,0:T(8,128)S(1)}, f32[72,320]{1,0:T(8,128)S(1)}, u32[]{:S(2)}, u32[]{:S(2)}) collective-permute-start(f32[72,320]{1,0:T(8,128)S(1)} %get-tuple-element.54.refs_7_), channel_id=1, source_target_pairs={{0,24},{4,28},{8,16},{12,20},{16,8},{20,12},{24,0},{28,4},{1,25},{... | collective-permute-start | bytes 276488 | tf_op jit(solution)/shard_map/ppermute | solution.py:25
  31.6 4.9 %collective-permute-start.3 = (f32[72,320]{1,0:T(8,128)S(1)}, f32[72,320]{1,0:T(8,128)S(1)}, u32[]{:S(2)}, u32[]{:S(2)}) collective-permute-start(f32[72,320]{1,0:T(8,128)S(1)} %get-tuple-element.54.refs_7_), channel_id=1, source_target_pairs={{0,16},{4,20},{8,24},{12,28},{16,0},{20,4},{24,8},{28,12},{1,17},{... | collective-permute-start | bytes 276488 | tf_op jit(solution)/shard_map/ppermute | solution.py:25
  32.1 4.7 %collective-permute-start.4 = (f32[72,320]{1,0:T(8,128)S(1)}, f32[72,320]{1,0:T(8,128)S(1)}, u32[]{:S(2)}, u32[]{:S(2)}) collective-permute-start(f32[72,320]{1,0:T(8,128)S(1)} %get-tuple-element.54.refs_7_), channel_id=1, source_target_pairs={{0,8},{4,12},{8,0},{12,4},{16,24},{20,28},{24,16},{28,20},{1,9},{5... | collective-permute-start | bytes 276488 | tf_op jit(solution)/shard_map/ppermute | solution.py:25
  32.5 5.6 %collective-permute-start.5 = (f32[72,320]{1,0:T(8,128)S(1)}, f32[72,320]{1,0:T(8,128)S(1)}, u32[]{:S(2)}, u32[]{:S(2)}) collective-permute-start(f32[72,320]{1,0:T(8,128)S(1)} %get-tuple-element.54.refs_7_), channel_id=1, source_target_pairs={{0,4},{4,0},{8,12},{12,8},{16,20},{20,16},{24,28},{28,24},{1,5},{5... | collective-permute-start | bytes 276488 | tf_op jit(solution)/shard_map/ppermute | solution.py:25
  35.2 2.9 %collective-permute-start.6 = (f32[72,320]{1,0:T(8,128)S(1)}, f32[72,320]{1,0:T(8,128)S(1)}, u32[]{:S(2)}, u32[]{:S(2)}) collective-permute-start(f32[72,320]{1,0:T(8,128)S(1)} %collective-permute-done.2.refs_0_), channel_id=1, source_target_pairs={{0,4},{4,0},{8,12},{12,8},{16,20},{20,16},{24,28},{28,24},{1,5},{5... | collective-permute-start | bytes 276488 | tf_op jit(solution)/shard_map/ppermute | solution.py:25
  36.5 1.7 %collective-permute-start.7 = (f32[72,320]{1,0:T(8,128)S(1)}, f32[72,320]{1,0:T(8,128)S(1)}, u32[]{:S(2)}, u32[]{:S(2)}) collective-permute-start(f32[72,320]{1,0:T(8,128)S(1)} %collective-permute-done.3.refs_1_), channel_id=1, source_target_pairs={{0,4},{4,0},{8,12},{12,8},{16,20},{20,16},{24,28},{28,24},{1,5},{5... | collective-permute-start | bytes 276488 | tf_op jit(solution)/shard_map/ppermute | solution.py:25
  36.9 1.3 %collective-permute-start.8 = (f32[72,320]{1,0:T(8,128)S(1)}, f32[72,320]{1,0:T(8,128)S(1)}, u32[]{:S(2)}, u32[]{:S(2)}) collective-permute-start(f32[72,320]{1,0:T(8,128)S(1)} %collective-permute-done.4.refs_2_), channel_id=1, source_target_pairs={{0,4},{4,0},{8,12},{12,8},{16,20},{20,16},{24,28},{28,24},{1,5},{5... | collective-permute-start | bytes 276488 | tf_op jit(solution)/shard_map/ppermute | solution.py:25
  40.4 1.9 %collective-permute-start.9 = (bf16[384,640]{1,0:T(8,128)(2,1)S(1)}, bf16[384,640]{1,0:T(8,128)(2,1)S(1)}, u32[]{:S(2)}, u32[]{:S(2)}) collective-permute-start(bf16[384,640]{1,0:T(8,128)(2,1)S(1)} %get-tuple-element.64), channel_id=1, source_target_pairs={{0,4},{4,0},{8,12},{12,8},{16,20},{20,16},{24,28},{28,24},{1,5},{5... | collective-permute-start | bytes 1474568 | tf_op jit(solution)/shard_map/ppermute | solution.py:25
  46.5 16.0 %collective-permute-start.23 = (bf16[384,640]{1,0:T(8,128)(2,1)S(1)}, bf16[384,640]{1,0:T(8,128)(2,1)S(1)}, u32[]{:S(2)}, u32[]{:S(2)}) collective-permute-start(bf16[384,640]{1,0:T(8,128)(2,1)S(1)} %get-tuple-element.82), channel_id=1, source_target_pairs={{0,4},{4,0},{8,12},{12,8},{16,20},{20,16},{24,28},{28,24},{1,5},{5... | collective-permute-start | bytes 1474568 | tf_op jit(solution)/shard_map/ppermute | solution.py:25
  46.9 7.1 %collective-permute-start.10 = (bf16[96,640]{1,0:T(8,128)(2,1)S(1)}, bf16[96,640]{1,0:T(8,128)(2,1)S(1)}, u32[]{:S(2)}, u32[]{:S(2)}) collective-permute-start(bf16[96,640]{1,0:T(8,128)(2,1)S(1)} %get-tuple-element.66), channel_id=1, source_target_pairs={{0,24},{4,28},{8,16},{12,20},{16,8},{20,12},{24,0},{28,4},{1,25},{... | collective-permute-start | bytes 368648 | tf_op jit(solution)/shard_map/ppermute | solution.py:25
  48.5 7.4 %collective-permute-start.11 = (bf16[96,640]{1,0:T(8,128)(2,1)S(1)}, bf16[96,640]{1,0:T(8,128)(2,1)S(1)}, u32[]{:S(2)}, u32[]{:S(2)}) collective-permute-start(bf16[96,640]{1,0:T(8,128)(2,1)S(1)} %get-tuple-element.67), channel_id=1, source_target_pairs={{0,16},{4,20},{8,24},{12,28},{16,0},{20,4},{24,8},{28,12},{1,17},{... | collective-permute-start | bytes 368648 | tf_op jit(solution)/shard_map/ppermute | solution.py:25
  49.6 6.4 %collective-permute-start.12 = (bf16[96,640]{1,0:T(8,128)(2,1)S(1)}, bf16[96,640]{1,0:T(8,128)(2,1)S(1)}, u32[]{:S(2)}, u32[]{:S(2)}) collective-permute-start(bf16[96,640]{1,0:T(8,128)(2,1)S(1)} %get-tuple-element.68), channel_id=1, source_target_pairs={{0,8},{4,12},{8,0},{12,4},{16,24},{20,28},{24,16},{28,20},{1,9},{5... | collective-permute-start | bytes 368648 | tf_op jit(solution)/shard_map/ppermute | solution.py:25
  56.0 9.3 %collective-permute-start.13 = (bf16[24,640]{1,0:T(8,128)(2,1)S(1)}, bf16[24,640]{1,0:T(8,128)(2,1)S(1)}, u32[]{:S(2)}, u32[]{:S(2)}) collective-permute-start(bf16[24,640]{1,0:T(8,128)(2,1)S(1)} %get-tuple-element.70), channel_id=1, source_target_pairs={{0,3},{1,2},{2,1},{3,0},{4,7},{5,6},{6,5},{7,4},{8,11},{9,10},{10,... | collective-permute-start | bytes 92168 | tf_op jit(solution)/shard_map/ppermute | solution.py:25
  59.7 6.6 %collective-permute-start.14 = (bf16[24,640]{1,0:T(8,128)(2,1)S(1)}, bf16[24,640]{1,0:T(8,128)(2,1)S(1)}, u32[]{:S(2)}, u32[]{:S(2)}) collective-permute-start(bf16[24,640]{1,0:T(8,128)(2,1)S(1)} %get-tuple-element.71), channel_id=1, source_target_pairs={{0,2},{1,3},{2,0},{3,1},{4,6},{5,7},{6,4},{7,5},{8,10},{9,11},{10,... | collective-permute-start | bytes 92168 | tf_op jit(solution)/shard_map/ppermute | solution.py:25
  62.1 4.1 %collective-permute-start.15 = (bf16[24,640]{1,0:T(8,128)(2,1)S(1)}, bf16[24,640]{1,0:T(8,128)(2,1)S(1)}, u32[]{:S(2)}, u32[]{:S(2)}) collective-permute-start(bf16[24,640]{1,0:T(8,128)(2,1)S(1)} %get-tuple-element.72), channel_id=1, source_target_pairs={{0,1},{1,0},{2,3},{3,2},{4,5},{5,4},{6,7},{7,6},{8,9},{9,8},{10,11... | collective-permute-start | bytes 92168 | tf_op jit(solution)/shard_map/ppermute | solution.py:25
  62.7 38.2 %copy-start.4 = (bf16[641,72]{0,1:T(8,128)(2,1)S(1)}, bf16[641,72]{0,1:T(8,128)(2,1)}, u32[]{:S(2)}) copy-start(bf16[641,72]{0,1:T(8,128)(2,1)} %param.13) | copy-start | bytes 276916
  62.7 14.8 %collective-permute-start.24 = (bf16[96,640]{1,0:T(8,128)(2,1)S(1)}, bf16[96,640]{1,0:T(8,128)(2,1)S(1)}, u32[]{:S(2)}, u32[]{:S(2)}) collective-permute-start(bf16[96,640]{1,0:T(8,128)(2,1)S(1)} %get-tuple-element.84), channel_id=1, source_target_pairs={{0,24},{4,28},{8,16},{12,20},{16,8},{20,12},{24,0},{28,4},{1,25},{... | collective-permute-start | bytes 368648 | tf_op jit(solution)/shard_map/ppermute | solution.py:25
  64.1 13.3 %collective-permute-start.25 = (bf16[96,640]{1,0:T(8,128)(2,1)S(1)}, bf16[96,640]{1,0:T(8,128)(2,1)S(1)}, u32[]{:S(2)}, u32[]{:S(2)}) collective-permute-start(bf16[96,640]{1,0:T(8,128)(2,1)S(1)} %get-tuple-element.85), channel_id=1, source_target_pairs={{0,16},{4,20},{8,24},{12,28},{16,0},{20,4},{24,8},{28,12},{1,17},{... | collective-permute-start | bytes 368648 | tf_op jit(solution)/shard_map/ppermute | solution.py:25
  65.3 12.1 %collective-permute-start.26 = (bf16[96,640]{1,0:T(8,128)(2,1)S(1)}, bf16[96,640]{1,0:T(8,128)(2,1)S(1)}, u32[]{:S(2)}, u32[]{:S(2)}) collective-permute-start(bf16[96,640]{1,0:T(8,128)(2,1)S(1)} %get-tuple-element.86), channel_id=1, source_target_pairs={{0,8},{4,12},{8,0},{12,4},{16,24},{20,28},{24,16},{28,20},{1,9},{5... | collective-permute-start | bytes 368648 | tf_op jit(solution)/shard_map/ppermute | solution.py:25
  66.3 5.8 %collective-permute-start.16 = (bf16[24,640]{1,0:T(8,128)(2,1)S(1)}, bf16[24,640]{1,0:T(8,128)(2,1)S(1)}, u32[]{:S(2)}, u32[]{:S(2)}) collective-permute-start(bf16[24,640]{1,0:T(8,128)(2,1)S(1)} %shard_map.134.own_ref), channel_id=1, source_target_pairs={{0,3},{1,2},{2,1},{3,0},{4,7},{5,6},{6,5},{7,4},{8,11},{9,10},{10,... | collective-permute-start | bytes 92168 | tf_op jit(solution)/shard_map/ppermute | solution.py:25
  68.8 4.8 %collective-permute-start.17 = (bf16[24,640]{1,0:T(8,128)(2,1)S(1)}, bf16[24,640]{1,0:T(8,128)(2,1)S(1)}, u32[]{:S(2)}, u32[]{:S(2)}) collective-permute-start(bf16[24,640]{1,0:T(8,128)(2,1)S(1)} %shard_map.134.own_ref), channel_id=1, source_target_pairs={{0,2},{1,3},{2,0},{3,1},{4,6},{5,7},{6,4},{7,5},{8,10},{9,11},{10,... | collective-permute-start | bytes 92168 | tf_op jit(solution)/shard_map/ppermute | solution.py:25
  72.1 3.9 %collective-permute-start.18 = (bf16[24,640]{1,0:T(8,128)(2,1)S(1)}, bf16[24,640]{1,0:T(8,128)(2,1)S(1)}, u32[]{:S(2)}, u32[]{:S(2)}) collective-permute-start(bf16[24,640]{1,0:T(8,128)(2,1)S(1)} %shard_map.134.own_ref), channel_id=1, source_target_pairs={{0,1},{1,0},{2,3},{3,2},{4,5},{5,4},{6,7},{7,6},{8,9},{9,8},{10,11... | collective-permute-start | bytes 92168 | tf_op jit(solution)/shard_map/ppermute | solution.py:25
  76.0 19.8 %collective-permute-start.19 = (bf16[96,640]{1,0:T(8,128)(2,1)S(1)}, bf16[96,640]{1,0:T(8,128)(2,1)S(1)}, u32[]{:S(2)}, u32[]{:S(2)}) collective-permute-start(bf16[96,640]{1,0:T(8,128)(2,1)S(1)} %bitcast.25), channel_id=1, source_target_pairs={{0,24},{4,28},{8,16},{12,20},{16,8},{20,12},{24,0},{28,4},{1,25},{... | collective-permute-start | bytes 368648 | tf_op jit(solution)/shard_map/ppermute | solution.py:25
  77.5 5.8 %collective-permute-start.27 = (bf16[24,640]{1,0:T(8,128)(2,1)S(1)}, bf16[24,640]{1,0:T(8,128)(2,1)S(1)}, u32[]{:S(2)}, u32[]{:S(2)}) collective-permute-start(bf16[24,640]{1,0:T(8,128)(2,1)S(1)} %get-tuple-element.88), channel_id=1, source_target_pairs={{0,3},{1,2},{2,1},{3,0},{4,7},{5,6},{6,5},{7,4},{8,11},{9,10},{10,... | collective-permute-start | bytes 92168 | tf_op jit(solution)/shard_map/ppermute | solution.py:25
  80.4 5.5 %collective-permute-start.28 = (bf16[24,640]{1,0:T(8,128)(2,1)S(1)}, bf16[24,640]{1,0:T(8,128)(2,1)S(1)}, u32[]{:S(2)}, u32[]{:S(2)}) collective-permute-start(bf16[24,640]{1,0:T(8,128)(2,1)S(1)} %get-tuple-element.89), channel_id=1, source_target_pairs={{0,2},{1,3},{2,0},{3,1},{4,6},{5,7},{6,4},{7,5},{8,10},{9,11},{10,... | collective-permute-start | bytes 92168 | tf_op jit(solution)/shard_map/ppermute | solution.py:25
  80.4 5.5 %collective-permute-start.29 = (bf16[24,640]{1,0:T(8,128)(2,1)S(1)}, bf16[24,640]{1,0:T(8,128)(2,1)S(1)}, u32[]{:S(2)}, u32[]{:S(2)}) collective-permute-start(bf16[24,640]{1,0:T(8,128)(2,1)S(1)} %get-tuple-element.90), channel_id=1, source_target_pairs={{0,1},{1,0},{2,3},{3,2},{4,5},{5,4},{6,7},{7,6},{8,9},{9,8},{10,11... | collective-permute-start | bytes 92168 | tf_op jit(solution)/shard_map/ppermute | solution.py:25
  86.0 5.8 %collective-permute-start.30 = (bf16[24,640]{1,0:T(8,128)(2,1)S(1)}, bf16[24,640]{1,0:T(8,128)(2,1)S(1)}, u32[]{:S(2)}, u32[]{:S(2)}) collective-permute-start(bf16[24,640]{1,0:T(8,128)(2,1)S(1)} %shard_map.142.own_ref), channel_id=1, source_target_pairs={{0,3},{1,2},{2,1},{3,0},{4,7},{5,6},{6,5},{7,4},{8,11},{9,10},{10,... | collective-permute-start | bytes 92168 | tf_op jit(solution)/shard_map/ppermute | solution.py:25
  88.0 5.4 %collective-permute-start.31 = (bf16[24,640]{1,0:T(8,128)(2,1)S(1)}, bf16[24,640]{1,0:T(8,128)(2,1)S(1)}, u32[]{:S(2)}, u32[]{:S(2)}) collective-permute-start(bf16[24,640]{1,0:T(8,128)(2,1)S(1)} %shard_map.142.own_ref), channel_id=1, source_target_pairs={{0,2},{1,3},{2,0},{3,1},{4,6},{5,7},{6,4},{7,5},{8,10},{9,11},{10,... | collective-permute-start | bytes 92168 | tf_op jit(solution)/shard_map/ppermute | solution.py:25
  88.0 5.4 %collective-permute-start.32 = (bf16[24,640]{1,0:T(8,128)(2,1)S(1)}, bf16[24,640]{1,0:T(8,128)(2,1)S(1)}, u32[]{:S(2)}, u32[]{:S(2)}) collective-permute-start(bf16[24,640]{1,0:T(8,128)(2,1)S(1)} %shard_map.142.own_ref), channel_id=1, source_target_pairs={{0,1},{1,0},{2,3},{3,2},{4,5},{5,4},{6,7},{7,6},{8,9},{9,8},{10,11... | collective-permute-start | bytes 92168 | tf_op jit(solution)/shard_map/ppermute | solution.py:25
  90.4 6.6 %collective-permute-start.20 = (bf16[96,640]{1,0:T(8,128)(2,1)S(1)}, bf16[96,640]{1,0:T(8,128)(2,1)S(1)}, u32[]{:S(2)}, u32[]{:S(2)}) collective-permute-start(bf16[96,640]{1,0:T(8,128)(2,1)S(1)} %bitcast.26), channel_id=1, source_target_pairs={{0,16},{4,20},{8,24},{12,28},{16,0},{20,4},{24,8},{28,12},{1,17},{... | collective-permute-start | bytes 368648 | tf_op jit(solution)/shard_map/ppermute | solution.py:25
  91.7 5.3 %collective-permute-start.21 = (bf16[96,640]{1,0:T(8,128)(2,1)S(1)}, bf16[96,640]{1,0:T(8,128)(2,1)S(1)}, u32[]{:S(2)}, u32[]{:S(2)}) collective-permute-start(bf16[96,640]{1,0:T(8,128)(2,1)S(1)} %bitcast.27), channel_id=1, source_target_pairs={{0,8},{4,12},{8,0},{12,4},{16,24},{20,28},{24,16},{28,20},{1,9},{5... | collective-permute-start | bytes 368648 | tf_op jit(solution)/shard_map/ppermute | solution.py:25
  93.4 5.9 %collective-permute-start.33 = (bf16[96,640]{1,0:T(8,128)(2,1)S(1)}, bf16[96,640]{1,0:T(8,128)(2,1)S(1)}, u32[]{:S(2)}, u32[]{:S(2)}) collective-permute-start(bf16[96,640]{1,0:T(8,128)(2,1)S(1)} %bitcast.29), channel_id=1, source_target_pairs={{0,24},{4,28},{8,16},{12,20},{16,8},{20,12},{24,0},{28,4},{1,25},{... | collective-permute-start | bytes 368648 | tf_op jit(solution)/shard_map/ppermute | solution.py:25
  94.5 6.1 %collective-permute-start.34 = (bf16[96,640]{1,0:T(8,128)(2,1)S(1)}, bf16[96,640]{1,0:T(8,128)(2,1)S(1)}, u32[]{:S(2)}, u32[]{:S(2)}) collective-permute-start(bf16[96,640]{1,0:T(8,128)(2,1)S(1)} %bitcast.30), channel_id=1, source_target_pairs={{0,16},{4,20},{8,24},{12,28},{16,0},{20,4},{24,8},{28,12},{1,17},{... | collective-permute-start | bytes 368648 | tf_op jit(solution)/shard_map/ppermute | solution.py:25
  95.9 4.9 %collective-permute-start.35 = (bf16[96,640]{1,0:T(8,128)(2,1)S(1)}, bf16[96,640]{1,0:T(8,128)(2,1)S(1)}, u32[]{:S(2)}, u32[]{:S(2)}) collective-permute-start(bf16[96,640]{1,0:T(8,128)(2,1)S(1)} %bitcast.31), channel_id=1, source_target_pairs={{0,8},{4,12},{8,0},{12,4},{16,24},{20,28},{24,16},{28,20},{1,9},{5... | collective-permute-start | bytes 368648 | tf_op jit(solution)/shard_map/ppermute | solution.py:25
  97.1 4.0 %collective-permute-start.22 = (bf16[384,640]{1,0:T(8,128)(2,1)S(1)}, bf16[384,640]{1,0:T(8,128)(2,1)S(1)}, u32[]{:S(2)}, u32[]{:S(2)}) collective-permute-start(bf16[384,640]{1,0:T(8,128)(2,1)S(1)} %bitcast.17), channel_id=1, source_target_pairs={{0,4},{4,0},{8,12},{12,8},{16,20},{20,16},{24,28},{28,24},{1,5},{5... | collective-permute-start | bytes 1474568 | tf_op jit(solution)/shard_map/ppermute | solution.py:25
  100.8 2.9 %collective-permute-start.36 = (bf16[384,640]{1,0:T(8,128)(2,1)S(1)}, bf16[384,640]{1,0:T(8,128)(2,1)S(1)}, u32[]{:S(2)}, u32[]{:S(2)}) collective-permute-start(bf16[384,640]{1,0:T(8,128)(2,1)S(1)} %bitcast.20), channel_id=1, source_target_pairs={{0,4},{4,0},{8,12},{12,8},{16,20},{20,16},{24,28},{28,24},{1,5},{5... | collective-permute-start | bytes 1474568 | tf_op jit(solution)/shard_map/ppermute | solution.py:25
